TPU v7x, 32 devices: a whole 2x2x4 slice. The times are simulated.
32 devices in a mesh: dp: 4 (over y, core), seq: 8 (over z, x).
Axes of the slice: x: 2, y: 2, z: 4, core: 2. Of those that a mesh axis runs over, the one named last changes fastest.
Arguments:
- head_inputs: bfloat16 [4, 3072, 1024], P('dp', 'seq'), may hold values from -6 to 6
- gate_inputs: bfloat16 [4, 3072, 1024], P('dp', 'seq'), may hold values from -6 to 6
- state_proj: bfloat16 [4, 3072, 256], P('dp', 'seq'), may hold values from -2 to 2
- time_steps: float32 [4, 3072, 16], P('dp', 'seq'), may hold values from -4.7 to 4.7
- token_ids: int32 [4, 3072], P('dp', 'seq'), may hold values from 0 to 50279, as said below
- token_counts: int32 [4], replicated, may hold values from 1536 to 3072
- teacher_out: bfloat16 [4, 3072, 1024], P('dp', 'seq'), may hold values from -6 to 6
- out_weight: float32 [1024, 1024], P(('dp', 'seq')), may hold values from -0.1875 to 0.1875
- decay_log: float32 [16], replicated, may hold values from -6.5 to 1
- step_bias: float32 [16], replicated, may hold values from -5 to -3
- skip_gain: float32 [16], replicated, may hold values from 0.5 to 1.5
- norm_gain: float32 [1024], replicated, may hold values from 0.5 to 1.5
Outputs:
- losses: float32 [2], replicated
- new_weight: float32 [1024, 1024], P(('dp', 'seq'))
- new_decay: float32 [16], replicated
- new_bias: float32 [16], replicated
- new_skip: float32 [16], replicated
- new_gain: float32 [1024], replicated
Inputs may be any that keep to these rules, and one draw needn't show every extreme that they name: `token_ids`: in each sequence exactly one position, never the first, holds id 0.
All inputs are finite; a program needn't handle non-finite values.
Results may differ from a plain program's by a relative error of at most 0.0003.
Values may be sent and summed in bfloat16 or wider, within the bound.
A program may use at most 192 MiB of HBM per device.

v0:
```python
import jax
import jax.numpy as jnp
from jax import lax
from jax.sharding import PartitionSpec as P

STEPS = 2


norm_floor = 1.0
clip_limit = 1.0
learn_rate = 8.0
highest = lax.Precision.HIGHEST
masked_low = -10000.0


def prefix(part, axis, combine, identity):
    place = lax.axis_index(axis)
    gathered = jax.tree.map(lambda a: lax.all_gather(a, axis), part)
    state = jax.tree.map(lambda a, e: jnp.zeros_like(a) + jnp.asarray(e, a.dtype), part, identity)

    def one(turn, state):
        return combine(
            state, jax.tree.map(lambda a: lax.dynamic_index_in_dim(a, turn, 0, False), gathered)
        )

    return lax.fori_loop(0, place, one, state)


def prefix_2(array, axis, join, neutral):
    count = lax.axis_size(axis)
    place = lax.axis_index(axis)
    ahead = count - 1 - place
    gathered = jax.tree.map(
        lambda a, kind: lax.all_gather(a.astype(kind), axis),
        array,
        jax.tree.map(lambda a: jnp.bfloat16 if a.dtype == jnp.float32 else a.dtype, array),
    )
    state = jax.tree.map(lambda a, e: jnp.zeros_like(a) + jnp.asarray(e, a.dtype), array, neutral)

    def one(turn, state):
        source = count - 1 - turn
        return join(
            state,
            jax.tree.map(
                lambda a, own: lax.dynamic_index_in_dim(a, source, 0, False).astype(own.dtype),
                gathered,
                array,
            ),
        )

    return lax.fori_loop(0, ahead, one, state)


def joined(part, axis, combine):
    gathered = jax.tree.map(lambda a: lax.all_gather(a, axis), part)

    def take(source):
        return jax.tree.map(lambda a: lax.dynamic_index_in_dim(a, source, 0, False), gathered)

    return lax.fori_loop(
        1, lax.axis_size(axis), lambda source, state: combine(state, take(source)), take(0)
    )


def step_sizes(decay_log, step_bias, step_raw):
    step_width = jax.nn.softplus(step_raw + step_bias[None, :])
    decay_sum = jnp.cumsum(step_width * (-jnp.exp(decay_log))[None, :], axis=0)
    return (step_width, decay_sum)


def mix_block(
    decay_log,
    step_bias,
    skip_gain,
    norm_gain,
    state_in,
    head_inputs,
    gate_inputs,
    b_proj,
    c_proj,
    step_raw,
    segment,
):
    positions = head_inputs.shape[0]
    head_count = decay_log.shape[0]
    step_width, decay_sum = step_sizes(decay_log, step_bias, step_raw)
    inputs_f = head_inputs.astype(jnp.float32).reshape(positions, head_count, -1)
    scaled = inputs_f * step_width[:, :, None]
    scores = jnp.dot(c_proj, b_proj.T, preferred_element_type=jnp.float32)
    position = jnp.arange(positions)
    allowed = (segment[:, None] == segment[None, :]) & (position[:, None] >= position[None, :])

    def one_head(head_data):
        head_sum, head_scaled = head_data
        spread = head_sum[:, None] - head_sum[None, :]
        decay_grid = jnp.exp(jnp.where(allowed, spread, masked_low))
        return jnp.dot(decay_grid * scores, head_scaled, precision=highest)

    intra_sum = jnp.transpose(
        lax.map(one_head, (decay_sum.T, jnp.transpose(scaled, (1, 0, 2)))), (1, 0, 2)
    )
    entry_decay = jnp.exp(decay_sum) * (segment == 0)[:, None]
    carried = (
        jnp.einsum("in,hpn->ihp", c_proj.astype(jnp.float32), state_in, precision=highest)
        * entry_decay[:, :, None]
    )
    mixed_out = intra_sum + carried + skip_gain[None, :, None] * inputs_f
    gated = mixed_out.reshape(positions, -1) * jax.nn.silu(gate_inputs.astype(jnp.float32))
    mean_square = jnp.mean(gated * gated, axis=1, keepdims=True)
    return gated * norm_gain[None, :] * lax.rsqrt(mean_square + norm_floor)


def state_block(decay_log, step_bias, head_inputs, b_proj, step_raw, segment):
    positions = head_inputs.shape[0]
    head_count = decay_log.shape[0]
    step_width, decay_sum = step_sizes(decay_log, step_bias, step_raw)
    final_sum = decay_sum[-1]
    same_doc = (segment == segment[-1])[:, None]
    tail_decay = jnp.exp(jnp.where(same_doc, final_sum[None, :] - decay_sum, masked_low))
    inputs_f = head_inputs.astype(jnp.float32).reshape(positions, head_count, -1)
    weighted = inputs_f * (step_width * tail_decay)[:, :, None]
    state_out = jnp.einsum("jhp,jn->hpn", weighted, b_proj.astype(jnp.float32), precision=highest)
    carry_out = jnp.exp(final_sum) * (segment[-1] == 0)
    return (carry_out, state_out)


def combine_states(earlier, later):
    return (earlier[0] * later[0], later[0][:, None, None] * earlier[1] + later[1])


def combine_sums(first_part, second_part):
    summed_up = first_part[5] + second_part[5]
    back_part = summed_up - first_part[5]
    lost_part = first_part[5] - (summed_up - back_part) + (second_part[5] - back_part)
    grads_part = tuple(
        (left_item + right_item for left_item, right_item in zip(first_part[:5], second_part[:5]))
    )
    return grads_part + (summed_up, first_part[6] + second_part[6] + lost_part)


def per_device(
    head_inputs,
    gate_inputs,
    state_proj,
    time_steps,
    token_ids,
    token_counts,
    teacher_out,
    out_weight,
    decay_log,
    step_bias,
    skip_gain,
    norm_gain,
):
    tok_rows = head_inputs.shape[1]
    inner_width = head_inputs.shape[2]
    state_size = state_proj.shape[2] // 2
    model_width = teacher_out.shape[2]
    head_count = decay_log.shape[0]
    head_size = inner_width // head_count
    inputs_local = head_inputs[0]
    gates_local = gate_inputs[0]
    b_proj = state_proj[0, :, :state_size]
    c_proj = state_proj[0, :, state_size:]
    raw_local = time_steps[0]
    segment = jnp.cumsum((token_ids[0] == 0).astype(jnp.int32))
    position = lax.axis_index("seq") * tok_rows + jnp.arange(tok_rows, dtype=jnp.int32)
    own_count = lax.dynamic_index_in_dim(token_counts, lax.axis_index("dp"), keepdims=False)
    scored = (position < own_count).astype(jnp.float32)
    total_count = jnp.sum(token_counts).astype(jnp.float32)
    target_f = teacher_out[0].astype(jnp.float32)
    identity = (
        jnp.ones((head_count,), jnp.float32),
        jnp.zeros((head_count, head_size, state_size), jnp.float32),
    )
    losses = []
    for step_index in range(STEPS):
        weight_b = out_weight.astype(jnp.bfloat16)

        def state_part(decay_arg, bias_arg):
            return state_block(decay_arg, bias_arg, inputs_local, b_proj, raw_local, segment)

        (carry_out, state_out), state_pull = jax.vjp(state_part, decay_log, step_bias)
        state_in = prefix((carry_out, state_out), "seq", combine_states, identity)[1]

        def mix_part(decay_arg, bias_arg, skip_arg, gain_arg, entering):
            return mix_block(
                decay_arg,
                bias_arg,
                skip_arg,
                gain_arg,
                entering,
                inputs_local,
                gates_local,
                b_proj,
                c_proj,
                raw_local,
                segment,
            )

        normed, mix_pull = jax.vjp(mix_part, decay_log, step_bias, skip_gain, norm_gain, state_in)
        normed_b = normed.astype(jnp.bfloat16)
        output = jnp.dot(
            normed_b,
            lax.all_gather(weight_b, ("dp", "seq"), axis=0, tiled=True),
            preferred_element_type=jnp.float32,
        )
        residual = output - target_f
        token_loss = jnp.sum(residual * residual, axis=1) * scored / model_width
        loss_part = jnp.sum(token_loss)
        out_grad = (residual * (2.0 / (model_width * total_count)) * scored[:, None]).astype(
            jnp.bfloat16
        )
        weight_grad = jnp.dot(normed_b.T, out_grad, preferred_element_type=jnp.float32)
        normed_grad = jnp.dot(
            out_grad,
            lax.all_gather(weight_b, ("dp", "seq"), axis=0, tiled=True).T,
            preferred_element_type=jnp.float32,
        )
        decay_one, bias_one, skip_grad, gain_grad, state_grad = mix_pull(normed_grad)
        after_grad = prefix_2((carry_out, state_grad), "seq", combine_states, identity)[1]
        carry_grad = jnp.sum(after_grad * state_in, axis=(1, 2))
        decay_two, bias_two = state_pull((carry_grad, after_grad))
        decay_grad = decay_one + decay_two
        bias_grad = bias_one + bias_two
        grad_rows = lax.psum_scatter(weight_grad, ("dp", "seq"), scatter_dimension=0, tiled=True)
        merged = joined(
            (
                decay_grad,
                bias_grad,
                skip_grad,
                gain_grad,
                jnp.sum(grad_rows * grad_rows),
                loss_part,
                jnp.zeros((), jnp.float32),
            ),
            ("dp", "seq"),
            combine_sums,
        )
        decay_grad, bias_grad, skip_grad, gain_grad = (merged[0], merged[1], merged[2], merged[3])
        norm_square = (
            merged[4]
            + jnp.sum(decay_grad * decay_grad)
            + jnp.sum(bias_grad * bias_grad)
            + jnp.sum(skip_grad * skip_grad)
            + jnp.sum(gain_grad * gain_grad)
        )
        losses.append((merged[5] + merged[6]) / total_count)
        factor = clip_limit / jnp.maximum(jnp.sqrt(norm_square), clip_limit)
        out_weight = out_weight - learn_rate * factor * grad_rows
        decay_log = decay_log - learn_rate * factor * decay_grad
        step_bias = step_bias - learn_rate * factor * bias_grad
        skip_gain = skip_gain - learn_rate * factor * skip_grad
        norm_gain = norm_gain - learn_rate * factor * gain_grad
    return (jnp.stack(losses), out_weight, decay_log, step_bias, skip_gain, norm_gain)


def solution(mesh):
    in_specs = (
        P("dp", "seq", None),
        P("dp", "seq", None),
        P("dp", "seq", None),
        P("dp", "seq", None),
        P("dp", "seq"),
        P(),
        P("dp", "seq", None),
        P(("dp", "seq"), None),
        P(),
        P(),
        P(),
        P(),
    )
    out_specs = (P(), P(("dp", "seq"), None), P(), P(), P(), P())
    return jax.shard_map(
        per_device, mesh=mesh, in_specs=in_specs, out_specs=out_specs, check_vma=False
    )
```

profile of v0, /device:TPU:0, one launch (start us, length us, event | category | flops | bytes accessed | tf_op | source)
XLA Modules:
  0.0 1180.5 jit_solution(14342196870966235500)
XLA Ops:
  17.6 2.9 convert_multiply_fusion.1
  26.7 3.3 copy.164
  31.3 4.7 broadcast.372.clone
  36.0 4.6 broadcast.372.clone.1
  40.7 71.9 %while.178 = (s32[]{:T(128)}, f32[16,384,64]{1,2,0:T(8,128)}, f32[16,384,384]{2,1,0:T(8,128)}, f32[16,384,384]{2,1,0:T(8,128)}, f32[16,384]{1,0:T(8,128)}, /*ind...) while((s32[]{:T(128)}, f32[16,384,64]{1,2,0:T(8,128)}, ...), condition=%wide.region_7.9_spmd.clone, body=%wide.region_6.8_spmd.clone.sunk | while | flops 115015680 | bytes 2674797 | solution.py:100
  45.9 2.5 fusion.225
  50.4 2.5 fusion.225
  59.4 2.5 fusion.225
  86.3 2.5 fusion.225
  99.8 2.5 fusion.225
  104.3 2.5 fusion.225
  108.8 2.5 fusion.225
  117.2 3.1 copy.172
  120.3 22.9 %all-gather.12 = f32[8,1,16]{2,1,0:T(1,128)} all-gather(f32[1,1,16]{2,1,0:T(1,128)S(1)} %bitcast.743), channel_id=1, replica_groups=mesh['dp'=4,'seq'=8] {'seq'}, dimensions={0}, use_global_device_ids=true | all-gather | bytes 576 | tf_op jit(solution)/shard_map/all_gather | solution.py:18
  145.0 5.4 multiply_reduce_fusion.7
  150.4 3.1 copy.165
  153.5 4.8 all-gather.23.cloned.1.call-done
  158.3 4.2 multiply_reduce_fusion.4
  168.3 3.1 copy.173
  171.3 2.9 convolution_convert_fusion.1
  174.5 24.5 %all-gather.13 = bf16[8,1,16]{2,1,0:T(2,128)(2,1)S(1)} all-gather(bf16[1,1,16]{2,1,0:T(2,128)(2,1)S(1)} %bitcast.745), channel_id=1, replica_groups=mesh['dp'=4,'seq'=8] {'seq'}, dimensions={0}, use_global_device_ids=true | all-gather | bytes 288 | tf_op jit(solution)/shard_map/all_gather | solution.py:34
  200.7 3.1 copy.167
  203.7 5.5 fusion.167
  210.6 71.1 %while.179 = (s32[]{:T(128)}, f32[16,384]{1,0:T(8,128)S(1)}, f32[16,384,64]{1,2,0:T(8,128)}, f32[16,384,64]{1,2,0:T(8,128)}, f32[16,384,64]{2,1,0:T(8,128)}, /*i...) while((s32[]{:T(128)}, f32[16,384]{1,0:T(8,128)S(1)}, ...), condition=%wide.region_15.17_spmd.clone, body=%wide.region_12.16_spmd.clone.sunk | while | flops 227672064 | bytes 2282125 | solution.py:100
  281.7 64.7 %all-gather.5 = f32[32768]{0:T(1024)S(1)} all-gather(f32[1024]{0:T(1024)S(1)} %get-tuple-element.1776), channel_id=7, replica_groups=mesh['dp'=4,'seq'=8] {'dp','seq'}, dimensions={0}, use_global_device_ids=true | all-gather | bytes 135168 | tf_op jit(solution)/shard_map/all_gather | solution.py:55
  349.4 3.7 reduce-window.55
  359.5 8.1 while.173
  370.1 3.7 reduce-window.59
  378.1 37.4 %all-reduce.14 = (f32[512]{0:T(512)S(1)}, f32[512]{0:T(512)S(1)}, f32[512]{0:T(512)S(1)}, f32[32]{0:T(128)S(1)}, f32[32]{0:T(128)S(1)}, /*index=5*/f32[32]{0:T(128)S(1)}) all-reduce(f32[512]{0:T(512)S(1)} %multiply_dynamic-update-slice_fusion.1, f32[512]{0:T(512)S(1)} %add_dynamic-update-slice_fusion.1, ...), channel_id=4, replica_groups=mesh['dp'=4,'seq'=8] {'dp','seq'}, use_global_device_ids=true, to_apply=%add.2 | all-reduce | flops 1632 | bytes 13056
  415.9 161.9 %while.174 = (s32[]{:T(128)}, f32[16]{0:T(128)S(1)}, f32[16]{0:T(128)S(1)}, f32[16]{0:T(128)S(1)}, f32[1024]{0:T(1024)S(1)}, /*index=5*/f32[]{:T(128)}, f32[]{:T...) while((s32[]{:T(128)}, f32[16]{0:T(128)S(1)}, ...), condition=%wide.region_38.40_spmd, body=%wide.region_37.39_spmd.sunk | while | flops 1086 | bytes 21427 | solution.py:60
  586.3 3.1 copy.180
  589.4 2.9 convert_multiply_fusion
  592.3 3.1 copy.181
  595.4 3.0 fusion.108
  599.7 3.4 copy.182
  605.4 4.6 broadcast.372
  610.0 4.6 broadcast.372.clone.2
  614.6 60.6 %while.180 = (s32[]{:T(128)}, f32[16,384,64]{1,2,0:T(8,128)}, f32[16,384,384]{2,1,0:T(8,128)}, f32[16,384,384]{2,1,0:T(8,128)}, f32[16,384]{1,0:T(8,128)S(1)}, /...) while((s32[]{:T(128)}, f32[16,384,64]{1,2,0:T(8,128)}, ...), condition=%wide.region_48.50_spmd.clone, body=%wide.region_47.49_spmd.clone.sunk | while | flops 115015680 | bytes 2674797 | solution.py:100
  618.4 2.5 fusion.233
  629.8 2.5 fusion.233
  652.4 2.5 fusion.233
  660.0 2.5 fusion.233
  663.8 2.5 fusion.233
  667.6 2.5 fusion.233
  671.4 2.5 fusion.233
  676.5 3.1 copy.189
  679.5 20.8 %all-gather.14 = f32[8,1,16]{2,1,0:T(1,128)} all-gather(f32[1,1,16]{2,1,0:T(1,128)S(1)} %bitcast.744), channel_id=1, replica_groups=mesh['dp'=4,'seq'=8] {'seq'}, dimensions={0}, use_global_device_ids=true | all-gather | bytes 576 | tf_op jit(solution)/shard_map/all_gather | solution.py:18
  701.6 5.5 multiply_reduce_fusion.3
  707.1 3.1 copy.183
  711.3 19.0 %all-gather.25.cloned.1.call-done = bf16[1024,1024]{1,0:T(8,128)(2,1)} async-done(((bf16[32,1024]{1,0:T(8,128)(2,1)}), bf16[1024,1024]{1,0:T(8,128)(2,1)}) %all-gather.25.cloned.1.call-update) | async-done | bytes 2097168 | tf_op jit(solution)/shard_map/all_gather | solution.py:205
  730.4 4.5 multiply_reduce_fusion
  741.1 3.1 copy.190
  744.2 2.9 convolution_convert_fusion
  747.4 19.4 %all-gather.15 = bf16[8,1,16]{2,1,0:T(2,128)(2,1)S(1)} all-gather(bf16[1,1,16]{2,1,0:T(2,128)(2,1)S(1)} %bitcast.746), channel_id=1, replica_groups=mesh['dp'=4,'seq'=8] {'seq'}, dimensions={0}, use_global_device_ids=true | all-gather | bytes 288 | tf_op jit(solution)/shard_map/all_gather | solution.py:34
  766.9 3.1 copy.184
  769.9 65.1 %all-gather.11 = f32[32768]{0:T(1024)S(1)} all-gather(f32[1024]{0:T(1024)S(1)} %copy-done.62), channel_id=13, replica_groups=mesh['dp'=4,'seq'=8] {'dp','seq'}, dimensions={0}, use_global_device_ids=true | all-gather | bytes 135168 | tf_op jit(solution)/shard_map/all_gather | solution.py:55
  837.7 5.0 fusion.169
  844.1 71.2 %while.181 = (s32[]{:T(128)}, f32[16,384]{1,0:T(8,128)S(1)}, f32[16,384,64]{1,2,0:T(8,128)}, f32[16,384,64]{1,2,0:T(8,128)}, f32[16,384,64]{2,1,0:T(8,128)}, /*i...) while((s32[]{:T(128)}, f32[16,384]{1,0:T(8,128)S(1)}, ...), condition=%wide.region_55.57_spmd.clone, body=%wide.region_52.56_spmd.clone.sunk | while | flops 227672064 | bytes 2282125 | solution.py:100
  915.4 3.7 reduce-window.65
  923.5 8.1 while.176
  933.3 3.7 reduce-window.69
  937.7 47.6 %reduce-scatter.5.cloned.1.call-done = f32[32,1024]{1,0:T(8,128)} async-done(((f32[1024,1024]{1,0:T(8,128)}), f32[32,1024]{1,0:T(8,128)}) %reduce-scatter.5.cloned.1.call-update) | async-done | bytes 131088 | tf_op jit(solution)/shard_map/reduce_scatter | solution.py:226
  987.6 36.9 %all-reduce.13 = (f32[512]{0:T(512)S(1)}, f32[512]{0:T(512)S(1)}, f32[512]{0:T(512)S(1)}, f32[32]{0:T(128)S(1)}, f32[32]{0:T(128)S(1)}) all-reduce(f32[512]{0:T(512)S(1)} %multiply_dynamic-update-slice_fusion, f32[512]{0:T(512)S(1)} %add_dynamic-update-slice_fusion, ...), channel_id=10, replica_groups=mesh['dp'=4,'seq'=8] {'dp','seq'}, use_global_device_ids=true, to_apply=%add.8 | all-reduce | flops 1600 | bytes 12800
  1024.8 138.9 %while.177 = (s32[]{:T(128)}, f32[16]{0:T(128)S(1)}, f32[16]{0:T(128)S(1)}, f32[16]{0:T(128)S(1)}, f32[1024]{0:T(1024)S(1)}, /*index=5*/f32[]{:T(128)}, f32[]{:T...) while((s32[]{:T(128)}, f32[16]{0:T(128)S(1)}, ...), condition=%wide.region_78.80_spmd, body=%wide.region_77.79_spmd.sunk | while | flops 1086 | bytes 21427 | solution.py:60
  (1058 shorter events, 479.0 us)
Async XLA Ops:
  7.2 137.3 %all-gather.27.cloned.1.call-start = ((), (), s32[]{:S(2)}) async-start(), calls=%async_computation.6 | async-start | bytes 4718592 | tf_op jit(solution)/shard_map/all_gather | solution.py:18
  8.5 7.3 copy-start.32
  10.4 5.4 copy-start.37
  11.1 2.6 copy-start.63
  13.0 336.3 %copy-start.28 = (f32[16,4]{0,1:T(4,128)}, f32[16,4]{0,1:T(4,128)S(1)}, u32[]{:S(2)}) copy-start(f32[16,4]{0,1:T(4,128)S(1)} %reduce-window.50) | copy-start | bytes 772
  13.7 160.6 %copy-start.25 = (f32[384,16]{0,1:T(8,128)}, f32[384,16]{0,1:T(8,128)S(1)}, u32[]{:S(2)}) copy-start(f32[384,16]{0,1:T(8,128)S(1)} %get-tuple-element.2006) | copy-start | bytes 73732
  24.1 134.2 %all-gather.23.cloned.1.call-start = ((), (), s32[]{:S(2)}) async-start(), calls=%async_computation.2 | async-start | bytes 2162688 | tf_op jit(solution)/shard_map/all_gather | solution.py:205
  24.8 334.7 %all-gather.29.cloned.1.call-start = ((), (), s32[]{:S(2)}) async-start(), calls=%async_computation.7 | async-start | bytes 2359296 | tf_op jit(solution)/shard_map/all_gather | solution.py:34
  40.7 71.9 %copy-start.5 = (bf16[1,384,1024]{2,1,0:T(8,128)(2,1)S(1)}, bf16[1,384,1024]{2,1,0:T(8,128)(2,1)}, u32[]{:S(2)}) copy-start(bf16[1,384,1024]{2,1,0:T(8,128)(2,1)} %param.34) | copy-start | bytes 2359300
  112.6 3.3 copy-start.26
  117.2 3.1 copy-start.65
  150.4 3.1 copy-start.56
  150.4 7.9 copy-start.43
  153.5 9.0 copy-start.68
  158.2 4.2 copy-start.12
  158.3 4.2 copy-start.74
  164.2 2.7 copy-start.8
  174.2 201.6 %reduce-scatter.3.cloned.1.call-start = ((), (), s32[]{:S(2)}) async-start(), calls=%async_computation.3 | async-start | bytes 4325376 | tf_op jit(solution)/shard_map/reduce_scatter | solution.py:226
  200.6 3.1 copy-start.69
  209.2 492.3 %all-gather.31.cloned.1.call-start = ((), (), s32[]{:S(2)}) async-start(), calls=%async_computation.8 | async-start | bytes 4718592 | tf_op jit(solution)/shard_map/all_gather | solution.py:18
  346.4 2.9 copy-start.23
  347.1 6.7 copy-start.45
  347.1 6.9 copy-start.67
  359.5 8.2 copy-start.14
  367.7 48.2 %slice-start = ((f32[32768]{0:T(1024)}), f32[1024]{0:T(1024)S(1)}, s32[]{:S(2)}) async-start(f32[32768]{0:T(1024)} %copy-done.23), calls=%async_computation.10 | async-start | bytes 8192 | tf_op jit(solution)/shard_map/jit(dynamic_index_in_dim)/dynamic_slice | solution.py:58
  368.6 7.1 copy-start.64
  368.6 9.5 copy-start.58
  368.6 214.3 %copy-start.48 = (f32[16]{0:T(128)S(1)}, f32[16]{0:T(128)}, u32[]{:S(2)}) copy-start(f32[16]{0:T(128)} %param.42) | copy-start | bytes 196
  368.6 216.3 %copy-start.39 = (pred[384]{0:T(512)(128)(4,1)S(1)}, pred[384]{0:T(512)(128)(4,1)}, u32[]{:S(2)}) copy-start(pred[384]{0:T(512)(128)(4,1)} %copy-done.37) | copy-start | bytes 1156
  577.8 8.5 copy-start.77
  582.9 3.4 copy-start.41
  584.6 4.8 copy-start.30
  585.0 90.2 %copy-start.27 = (f32[384,16]{0,1:T(8,128)}, f32[384,16]{0,1:T(8,128)S(1)}, u32[]{:S(2)}) copy-start(f32[384,16]{0,1:T(8,128)S(1)} %get-tuple-element.2004) | copy-start | bytes 73732
  586.3 3.1 copy-start.2
  592.3 3.1 copy-start.15
  598.4 132.0 %all-gather.25.cloned.1.call-start = ((), (), s32[]{:S(2)}) async-start(), calls=%async_computation.4 | async-start | bytes 2162688 | tf_op jit(solution)/shard_map/all_gather | solution.py:205
  599.7 3.4 copy-start.19
  599.7 3.4 copy-start.21
  603.8 319.7 %all-gather.33.cloned.1.call-start = ((), (), s32[]{:S(2)}) async-start(), calls=%async_computation.9 | async-start | bytes 2359296 | tf_op jit(solution)/shard_map/all_gather | solution.py:34
  676.5 23.9 %copy-start.73 = (f32[16]{0:T(128)S(1)}, f32[16]{0:T(128)}, u32[]{:S(2)}) copy-start(f32[16]{0:T(128)} %param.43) | copy-start | bytes 196
  676.5 24.4 %copy-start.44 = (f32[1024]{0:T(1024)S(1)}, f32[1024]{0:T(1024)}, u32[]{:S(2)}) copy-start(f32[1024]{0:T(1024)} %param.44) | copy-start | bytes 12292
  707.1 23.3 %copy-start.35 = (f32[1024]{0:T(1024)S(1)}, f32[1024]{0:T(1024)}, u32[]{:S(2)}) copy-start(f32[1024]{0:T(1024)} %multiply_subtract_fusion.3) | copy-start | bytes 12292
  730.4 4.5 copy-start.6
  730.4 4.5 copy-start.10
  730.4 4.5 copy-start.53
  730.4 4.5 copy-start.70
  730.4 4.5 copy-start.75
  737.0 2.7 copy-start.9
  741.1 3.1 copy-start.16
  744.2 3.0 copy-start.78
  747.1 238.2 %reduce-scatter.5.cloned.1.call-start = ((), (), s32[]{:S(2)}) async-start(), calls=%async_computation.5 | async-start | bytes 4325376 | tf_op jit(solution)/shard_map/reduce_scatter | solution.py:226
  766.8 3.1 copy-start.62
  835.0 2.6 copy-start.11
  844.1 71.2 %copy-start.31 = (f32[16,4]{0,1:T(4,128)S(1)}, f32[16,4]{0,1:T(4,128)}, u32[]{:S(2)}) copy-start(f32[16,4]{0,1:T(4,128)} %copy-done.30) | copy-start | bytes 772
  844.1 71.2 %copy-start.34 = (f32[384]{0:T(512)S(1)}, f32[384]{0:T(512)}, u32[]{:S(2)}) copy-start(f32[384]{0:T(512)} %copy-done.32) | copy-start | bytes 4612
  844.1 75.2 %copy-start.46 = (f32[1024]{0:T(1024)S(1)}, f32[1024]{0:T(1024)}, u32[]{:S(2)}) copy-start(f32[1024]{0:T(1024)} %get-tuple-element.1973) | copy-start | bytes 12292
  844.1 75.6 %copy-start.66 = (f32[384]{0:T(512)S(1)}, f32[384]{0:T(512)}, u32[]{:S(2)}) copy-start(f32[384]{0:T(512)} %get-tuple-element.2015) | copy-start | bytes 4612
  931.7 5.6 copy-start.60
  931.7 5.9 copy-start.61
  931.7 93.1 %slice-start.1 = ((f32[32768]{0:T(1024)}), f32[1024]{0:T(1024)S(1)}, s32[]{:S(2)}) async-start(f32[32768]{0:T(1024)} %copy-done.24), calls=%async_computation.11 | async-start | bytes 8192 | tf_op jit(solution)/shard_map/jit(dynamic_index_in_dim)/dynamic_slice | solution.py:58
  932.5 237.4 %copy-start.72 = (f32[16]{0:T(128)S(1)}, f32[16]{0:T(128)}, u32[]{:S(2)}) copy-start(f32[16]{0:T(128)} %multiply_subtract_fusion.7) | copy-start | bytes 196
  932.6 237.9 %copy-start.36 = (f32[1024]{0:T(1024)S(1)}, f32[1024]{0:T(1024)}, u32[]{:S(2)}) copy-start(f32[1024]{0:T(1024)} %multiply_subtract_fusion.3) | copy-start | bytes 12292
  932.6 239.1 %copy-start.20 = (f32[32,1024]{1,0:T(8,128)S(1)}, f32[32,1024]{1,0:T(8,128)}, u32[]{:S(2)}) copy-start(f32[32,1024]{1,0:T(8,128)} %param.40) | copy-start | bytes 393220
  932.6 239.1 %copy-start.22 = (f32[32,1024]{1,0:T(8,128)S(1)}, f32[32,1024]{1,0:T(8,128)}, u32[]{:S(2)}) copy-start(f32[32,1024]{1,0:T(8,128)} %reduce-scatter.3.cloned.1.call-done) | copy-start | bytes 393220
  (27 other events, 41.8 us)
Sparse Core Ops, SparseCore 0:
  24.2 75.5 all-gather.26
  103.3 54.8 all-gather.22
  174.3 54.1 all-gather.28
  230.6 143.3 reduce-scatter.2
  598.5 73.4 all-gather.30
  675.4 54.9 all-gather.24
  747.2 48.7 all-gather.32
  842.9 142.3 reduce-scatter.4
where the time goes:
time: 1200 us; the launch traced here: 1180 us
  blocking collectives  292 us (24%)
  matrix products  265 us (22%)
  local copies, waits for them, and re-layouts  232 us (19%)
  loops' own time  166 us (14%)
  other arithmetic  131 us (11%)
  waiting for transfers between devices  71.6 us (6%)
  between operations  22.6 us (2%)
    dot_general x96, matrix products, one_head(): return jnp.dot(decay_grid * scores, head_scaled, precision=highest)  219 us
    another operation x2, loops' own time, joined(): lax.fori_loop(1, lax.axis_size(axis), lambda source, state: combine(state...  164 us
    dynamic_slice x258, local copies, waits for them, and re-layouts, take(): lax.dynamic_index_in_dim(a, source, 0, False)  134 us
    all_gather x2, blocking collectives, joined(): gathered = jax.tree.map(lambda a: lax.all_gather(a, axis), part)  130 us
    unnamed x2, blocking collectives  74.3 us
    reduce_scatter x2, waiting for transfers between devices, per_device(): lax.psum_scatter(weight_grad, ('dp', 'seq'), scatter_dimension=0, tiled=T...  47.6 us
    all_gather x2, blocking collectives, prefix_2(): lax.all_gather(a.astype(kind), axis)  43.9 us
    all_gather x2, blocking collectives, prefix(): gathered = jax.tree.map(lambda a: lax.all_gather(a, axis), part)  43.7 us
  transfers between devices with their start and end apart: 8, of which 3 were waited for; matrix products, arithmetic and copies ran while one was open for 35% of the time, Pallas kernels for 0%

commit v1 on v0

v1 whole, which is shorter than its diff:
```python
import functools

import jax
import jax.numpy as jnp
from jax import lax
from jax.experimental import pallas as pl
from jax.experimental.pallas import tpu as pltpu
from jax.sharding import PartitionSpec as P

STEPS = 2
norm_floor = 1.0
clip_limit = 1.0
learn_rate = 8.0
highest = lax.Precision.HIGHEST
f32 = jnp.float32
bf16 = jnp.bfloat16
LANES = 128
VMEM = pl.BlockSpec(memory_space=pltpu.VMEM)
MESH = pl.DeviceIdType.MESH
LIMIT = 60 * 1024 * 1024


def dot(a, b, **kw):
    return jnp.dot(a, b, preferred_element_type=f32, **kw)


def spread_matrix(heads, width):
    size = width // heads
    lane = lax.broadcasted_iota(jnp.int32, (heads, width), 1)
    head = lax.broadcasted_iota(jnp.int32, (heads, width), 0)
    return ((lane >= head * size) & (lane < (head + 1) * size)).astype(bf16)


def split(a):
    high = a.astype(bf16)
    return high, (a - high.astype(f32)).astype(bf16)


def spread(a, ones):
    high, low = split(a)
    return dot(high, ones) + dot(low, ones)


def head_sum(a, ones):
    high, low = split(a)
    turn = (((1,), (1,)), ((), ()))
    one = functools.partial(
        lax.dot_general, dimension_numbers=turn, preferred_element_type=f32
    )
    return one(high, ones) + one(low, ones)


def column(row):
    n = row.shape[1]
    i = lax.broadcasted_iota(jnp.int32, (n, n), 0)
    j = lax.broadcasted_iota(jnp.int32, (n, n), 1)
    return jnp.sum(jnp.where(i == j, row, 0.0), axis=1, keepdims=True)


def gain_rows(width):
    return width // LANES


def state_kernel(
    pack, raw, raw_t, ids_c, ids_r, x, b_t, sums, sums_t, width, seg_c, seg_r, state, carry
):
    tokens, heads = raw.shape
    inner = x.shape[1]
    g = gain_rows(inner)
    ones = spread_matrix(heads, inner)
    rate_row = -jnp.exp(pack[g : g + 1, :heads])
    bias_row = pack[g + 1 : g + 2, :heads]
    w = jax.nn.softplus(raw[...] + bias_row)
    w_t = jax.nn.softplus(raw_t[...] + column(bias_row))
    i = lax.broadcasted_iota(jnp.int32, (tokens, tokens), 0)
    j = lax.broadcasted_iota(jnp.int32, (tokens, tokens), 1)
    lower = (i >= j).astype(f32)
    upper = (i <= j).astype(f32)
    s = dot(lower, w * rate_row, precision=highest)
    sums[...] = s
    sums_t[...] = dot(w_t * column(rate_row), upper, precision=highest)
    width[...] = w
    sc = jnp.sum(jnp.where((i >= j) & (ids_r[...] == 0), 1.0, 0.0), axis=1, keepdims=True)
    sr = jnp.sum(jnp.where((i <= j) & (ids_c[...] == 0), 1.0, 0.0), axis=0, keepdims=True)
    seg_c[...] = sc
    seg_r[...] = sr
    last = sc[tokens - 1 : tokens, :]
    final = s[tokens - 1 : tokens, :]
    tail = jnp.where(sc == last, jnp.exp(final - s), 0.0)
    weighted = (x[...].astype(f32) * spread(w * tail, ones)).astype(bf16)
    state[...] = dot(b_t[...], weighted).astype(bf16)
    kept = jnp.where(last == 0.0, jnp.exp(final), 0.0)
    carry[...] = spread(jnp.broadcast_to(kept, (8, heads)), ones)[0:1, :]


def mix_kernel(
    pack, sums, sums_t, width, seg_c, seg_r, x, z, b, c, b_t, c_t, target, weight, state,
    scored, scale,
    weight_grad, state_grad, row_dot, col_dot, small, loss,
    scaled, mixed, slope_b, prod,
):
    tokens, heads = sums.shape
    inner = x.shape[1]
    g = gain_rows(inner)
    per = LANES // (inner // heads)
    size = inner // heads
    ones = spread_matrix(heads, inner)
    s = sums[...]
    xf = x[...].astype(f32)
    scaled[...] = (xf * spread(width[...], ones)).astype(bf16)
    i = lax.broadcasted_iota(jnp.int32, (tokens, tokens), 0)
    j = lax.broadcasted_iota(jnp.int32, (tokens, tokens), 1)
    same = seg_c[...] == seg_r[...]
    scores = jnp.where(same & (i >= j), dot(c[...], b_t[...]), 0.0)
    entry = spread(jnp.where(seg_c[...] == 0.0, jnp.exp(s), 0.0), ones)
    mixed[...] = dot(c[...], state[...]) * entry
    lane = lax.broadcasted_iota(jnp.int32, (LANES, LANES), 1)
    for k in range(inner // LANES):
        cols = slice(k * LANES, (k + 1) * LANES)
        for at in range(0, tokens, LANES):
            rows = slice(at, at + LANES)
            end = at + LANES
            total = None
            for p in range(per):
                h = k * per + p
                gap = sums[rows, h : h + 1] - sums_t[h : h + 1, :end]
                grid = (jnp.exp(jnp.minimum(gap, 0.0)) * scores[rows, :end]).astype(bf16)
                part = dot(grid, scaled[:end, cols])
                total = part if total is None else jnp.where(lane < p * size, total, part)
            mixed[rows, cols] += total
    gain = jnp.concatenate([pack[k : k + 1, :] for k in range(g)], axis=1)
    skip = spread(jnp.broadcast_to(pack[g + 2 : g + 3, :heads], (8, heads)), ones)[0:1, :]
    zf = z[...].astype(f32)
    silu = zf * jax.nn.sigmoid(zf)
    gated = (mixed[...] + skip * xf) * silu
    root = lax.rsqrt(jnp.mean(gated * gated, axis=1, keepdims=True) + norm_floor)
    normed = (gated * gain * root).astype(bf16)
    residual = dot(normed, weight[...]) - target[...].astype(f32)
    token_loss = jnp.sum(residual * residual, axis=1, keepdims=True) * scored[...]
    loss[...] = jnp.sum(token_loss, axis=0, keepdims=True) / target.shape[1]
    out_grad = (residual * scale[...]).astype(bf16)
    weight_grad[...] = lax.dot_general(
        normed, out_grad, (((0,), (0,)), ((), ())), preferred_element_type=f32
    ).astype(bf16)
    normed_grad = lax.dot_general(
        out_grad, weight[...], (((1,), (1,)), ((), ())), preferred_element_type=f32
    )
    lifted = normed_grad * gated
    gain_grad = jnp.sum(lifted * root, axis=0, keepdims=True)
    inward = jnp.sum(lifted * gain, axis=1, keepdims=True) * (root * root * root / inner)
    dy = (normed_grad * gain * root - gated * inward) * silu
    small[0:1, :] = gain_grad
    small[1:2, :] = jnp.sum(dy * xf, axis=0, keepdims=True)
    row_dot[...] = head_sum(dy * mixed[...], ones)
    state_grad[...] = dot(c_t[...], (entry * dy).astype(bf16)).astype(bf16)
    slope_b[...] = dy.astype(bf16)
    scores_t = dot(b[...], c_t[...])
    same_t = (seg_c[...] == seg_r[...]) & (i <= j)
    scores_t = jnp.where(same_t, scores_t, 0.0)
    for k in range(inner // LANES):
        cols = slice(k * LANES, (k + 1) * LANES)
        for at in range(0, tokens, LANES):
            rows = slice(at, at + LANES)
            total = None
            for p in range(per):
                h = k * per + p
                gap = sums_t[h : h + 1, at:] - sums[rows, h : h + 1]
                grid = (jnp.exp(jnp.minimum(gap, 0.0)) * scores_t[rows, at:]).astype(bf16)
                part = dot(grid, slope_b[at:, cols])
                total = part if total is None else jnp.where(lane < p * size, total, part)
            prod[rows, cols] = total * x[rows, cols].astype(f32)
    col_dot[...] = head_sum(prod[...], ones)


def back_kernel(
    pack, raw, sums, width, seg_c, x, b, after, state, carry, row_dot, col_dot, small, loss,
    grad_rows, out,
):
    tokens, heads = sums.shape
    inner = x.shape[1]
    g = gain_rows(inner)
    ones = spread_matrix(heads, inner)
    s = sums[...]
    w = width[...]
    rate_row = -jnp.exp(pack[g : g + 1, :heads])
    bias_row = pack[g + 1 : g + 2, :heads]
    sc = seg_c[...]
    last = sc[tokens - 1 : tokens, :]
    final = s[tokens - 1 : tokens, :]
    tail = jnp.where(sc == last, jnp.exp(final - s), 0.0)
    pulled = head_sum(dot(b[...], after[...]) * x[...].astype(f32), ones) * tail
    moved = after[...].astype(f32) * state[...].astype(f32)
    both = jnp.concatenate(
        [
            jnp.sum(moved, axis=0, keepdims=True) * carry[...],
            small[1:2, :],
            jnp.zeros((6, inner), f32),
        ],
        axis=0,
    )
    both = head_sum(both, ones)
    col = col_dot[...] + pulled
    d_sums = row_dot[...] - w * col
    d_final = jnp.sum(w * pulled, axis=0, keepdims=True) + both[0:1, :]
    i = lax.broadcasted_iota(jnp.int32, (tokens, tokens), 0)
    j = lax.broadcasted_iota(jnp.int32, (tokens, tokens), 1)
    d_rate = dot((i <= j).astype(f32), d_sums, precision=highest) + d_final
    d_width = (col + rate_row * d_rate) * jax.nn.sigmoid(raw[...] + bias_row)
    rows = grad_rows[...]
    square = jnp.sum(jnp.sum(rows * rows, axis=1, keepdims=True), axis=0, keepdims=True)
    out[...] = jnp.zeros(out.shape, f32)
    for k in range(g):
        out[k : k + 1, :] = small[0:1, k * LANES : (k + 1) * LANES]
    out[g : g + 1, :heads] = rate_row * jnp.sum(d_rate * w, axis=0, keepdims=True)
    out[g + 1 : g + 2, :heads] = jnp.sum(d_width, axis=0, keepdims=True)
    out[g + 2 : g + 3, :heads] = both[1:2, :]
    out[g + 3 : g + 4, :] = jnp.broadcast_to(loss[...], (1, LANES))
    out[g + 4 : g + 5, :] = jnp.broadcast_to(square, (1, LANES))


def place(flat, n_seq):
    return (flat // n_seq, flat % n_seq)


def meet(n_dp, n_seq):
    n = n_dp * n_seq
    me = lax.axis_index("dp") * n_seq + lax.axis_index("seq")
    barrier = pltpu.get_barrier_semaphore()

    def one(t, _):
        pl.semaphore_signal(
            barrier, inc=1, device_id=place((me + t) % n, n_seq), device_id_type=MESH
        )
        return 0

    lax.fori_loop(1, n, one, 0)
    pl.semaphore_wait(barrier, n - 1)
    return me


def flat_copy(n, n_seq, me, t, source, target, send, recv):
    peer = (me + t) % n
    return pltpu.make_async_remote_copy(
        src_ref=source(peer),
        dst_ref=target.at[me],
        send_sem=send.at[t],
        recv_sem=recv.at[t],
        device_id=place(peer, n_seq),
        device_id_type=MESH,
    )


def flat_arrival(n, n_seq, me, t, source, target, send, recv):
    peer = (me + n - t) % n
    return pltpu.make_async_remote_copy(
        src_ref=source(peer),
        dst_ref=target.at[peer],
        send_sem=send.at[t],
        recv_sem=recv.at[t],
        device_id=place(peer, n_seq),
        device_id_type=MESH,
    )


def seq_copy(n_seq, t, source, target, send, recv):
    mine = lax.axis_index("seq")
    peer = (mine + t) % n_seq
    return pltpu.make_async_remote_copy(
        src_ref=source(peer),
        dst_ref=target.at[mine],
        send_sem=send.at[t],
        recv_sem=recv.at[t],
        device_id=(lax.axis_index("dp"), peer),
        device_id_type=MESH,
    )


def seq_arrival(n_seq, t, source, target, send, recv):
    mine = lax.axis_index("seq")
    peer = (mine + n_seq - t) % n_seq
    return pltpu.make_async_remote_copy(
        src_ref=source(peer),
        dst_ref=target.at[peer],
        send_sem=send.at[t],
        recv_sem=recv.at[t],
        device_id=(lax.axis_index("dp"), peer),
        device_id_type=MESH,
    )


def each(n, body):
    def one(t, _):
        body(t)
        return 0

    lax.fori_loop(1, n, one, 0)


def gather_kernel(
    n_dp, n_seq, rows_b, state, carry, full, entering, carries,
    landed, ready, w_send, w_recv, s_send, s_recv, c_send, c_recv, r_send, r_recv,
):
    n = n_dp * n_seq
    me = meet(n_dp, n_seq)
    mine = lax.axis_index("seq")
    first = (n_seq, lambda p: state.at[p], landed, s_send, s_recv)
    lead = (n_seq, lambda p: carry, carries, c_send, c_recv)
    second = (n_seq, lambda p: ready.at[p], entering, r_send, r_recv)
    whole = (lambda p: rows_b, full, w_send, w_recv)
    go = lambda a, t: (a[0], t) + a[1:]

    def start(t):
        seq_copy(*go(lead, t)).start()
        seq_copy(*go(first, t)).start()

    each(n_seq, start)
    each(n, lambda t: flat_copy(n, n_seq, me, t, *whole).start())
    full[me] = rows_b[...]
    carries[mine] = carry[...]
    landed[mine] = state[mine]

    def arrive(t):
        seq_arrival(*go(lead, t)).wait_recv()
        seq_arrival(*go(first, t)).wait_recv()

    each(n_seq, arrive)
    running = jnp.zeros(state.shape[1:], f32)
    for d in range(n_seq):
        ready[d] = running.astype(bf16)
        if d < n_seq - 1:
            running = carries[d] * running + landed[d].astype(f32)
    each(n_seq, lambda t: seq_copy(*go(second, t)).start())
    entering[mine] = ready[mine]
    each(n_seq, lambda t: seq_arrival(*go(second, t)).wait_recv())
    each(n, lambda t: flat_arrival(n, n_seq, me, t, *whole).wait_recv())

    def sent(t):
        seq_copy(*go(lead, t)).wait_send()
        seq_copy(*go(first, t)).wait_send()
        seq_copy(*go(second, t)).wait_send()

    each(n_seq, sent)
    each(n, lambda t: flat_copy(n, n_seq, me, t, *whole).wait_send())


def scatter_kernel(
    n_dp, n_seq, grad, state, carries, total, leaving,
    parts, landed, ready, w_send, w_recv, s_send, s_recv, r_send, r_recv,
):
    n = n_dp * n_seq
    me = meet(n_dp, n_seq)
    mine = lax.axis_index("seq")
    first = (n_seq, lambda p: state.at[p], landed, s_send, s_recv)
    second = (n_seq, lambda p: ready.at[p], leaving, r_send, r_recv)
    whole = (lambda p: grad.at[p], parts, w_send, w_recv)
    go = lambda a, t: (a[0], t) + a[1:]
    each(n_seq, lambda t: seq_copy(*go(first, t)).start())
    each(n, lambda t: flat_copy(n, n_seq, me, t, *whole).start())
    landed[mine] = state[mine]
    total[...] = grad[me].astype(f32)
    each(n_seq, lambda t: seq_arrival(*go(first, t)).wait_recv())
    running = jnp.zeros(state.shape[1:], f32)
    for d in reversed(range(n_seq)):
        ready[d] = running.astype(bf16)
        if d > 0:
            running = carries[d] * running + landed[d].astype(f32)
    each(n_seq, lambda t: seq_copy(*go(second, t)).start())
    leaving[mine] = ready[mine]

    def add(t):
        flat_arrival(n, n_seq, me, t, *whole).wait_recv()
        total[...] += parts[(me + n - t) % n].astype(f32)

    each(n, add)
    each(n_seq, lambda t: seq_arrival(*go(second, t)).wait_recv())

    def sent(t):
        seq_copy(*go(first, t)).wait_send()
        seq_copy(*go(second, t)).wait_send()

    each(n_seq, sent)
    each(n, lambda t: flat_copy(n, n_seq, me, t, *whole).wait_send())


def update_kernel(
    n_dp, n_seq, inner, part, pack, rows, grad_rows, new_pack, new_rows, rows_b, loss,
    parts, send, recv,
):
    n = n_dp * n_seq
    me = meet(n_dp, n_seq)
    whole = (lambda p: part, parts, send, recv)
    each(n, lambda t: flat_copy(n, n_seq, me, t, *whole).start())
    parts[me] = part[...]
    each(n, lambda t: flat_arrival(n, n_seq, me, t, *whole).wait_recv())
    g = gain_rows(inner)
    summed = lax.fori_loop(1, n, lambda k, acc: acc + parts[k], parts[0])
    at = lax.broadcasted_iota(jnp.int32, summed.shape, 0)
    grads = jnp.where(at < g + 3, summed, 0.0)
    lane_sum = jnp.sum(grads * grads, axis=0, keepdims=True)
    norm_square = jnp.sum(lane_sum, axis=1, keepdims=True) + summed[g + 4 : g + 5, 0:1]
    factor = clip_limit / jnp.maximum(jnp.sqrt(norm_square), clip_limit)
    new_pack[...] = pack[...] - learn_rate * factor * grads
    fresh = rows[...] - learn_rate * factor * grad_rows[...]
    new_rows[...] = fresh
    rows_b[...] = fresh.astype(bf16)
    loss[...] = summed[g + 3 : g + 4, :]
    each(n, lambda t: flat_copy(n, n_seq, me, t, *whole).wait_send())


def call(body, outs, scratch=(), collective=None):
    extra = {}
    if collective is not None:
        extra = {"collective_id": collective, "has_side_effects": True}

    def run(*args):
        return pl.pallas_call(
            body,
            out_shape=tuple(jax.ShapeDtypeStruct(*o) for o in outs),
            in_specs=[VMEM] * len(args),
            out_specs=tuple([VMEM] * len(outs)),
            scratch_shapes=list(scratch),
            compiler_params=pltpu.CompilerParams(vmem_limit_bytes=LIMIT, **extra),
        )(*args)

    return run


def per_device(
    n_dp,
    n_seq,
    head_inputs,
    gate_inputs,
    state_proj,
    time_steps,
    token_ids,
    token_counts,
    teacher_out,
    out_weight,
    decay_log,
    step_bias,
    skip_gain,
    norm_gain,
):
    n = n_dp * n_seq
    x, z, target, raw = head_inputs[0], gate_inputs[0], teacher_out[0], time_steps[0]
    tokens, inner = x.shape
    ns = state_proj.shape[2] // 2
    heads = decay_log.shape[0]
    model = target.shape[1]
    share = out_weight.shape[0]
    piece = ns // n_seq
    g = gain_rows(inner)
    pack_rows = -(-(g + 5) // 8) * 8
    b, c = state_proj[0, :, :ns], state_proj[0, :, ns:]
    both_t = state_proj[0].T
    b_t, c_t = both_t[:ns], both_t[ns:]
    raw_t = raw.T
    ids_r = token_ids
    ids_c = token_ids.reshape(tokens, 1)
    position = lax.axis_index("seq") * tokens + jnp.arange(tokens, dtype=jnp.int32)
    own_count = lax.dynamic_index_in_dim(token_counts, lax.axis_index("dp"), keepdims=False)
    scored = (position < own_count).astype(f32)[:, None]
    total_count = jnp.sum(token_counts).astype(f32)
    scale = scored * (2.0 / (model * total_count))
    wide = lambda a: jnp.pad(a, (0, LANES - heads))[None]
    pack = jnp.concatenate(
        [
            norm_gain.reshape(g, LANES),
            wide(decay_log),
            wide(step_bias),
            wide(skip_gain),
            jnp.zeros((pack_rows - g - 3, LANES), f32),
        ]
    )
    rows = out_weight
    rows_b = rows.astype(bf16)
    dma = pltpu.SemaphoreType.DMA
    losses = []
    per_head = ((tokens, heads), f32)
    for _ in range(STEPS):
        sums, sums_t, width, seg_c, seg_r, state, carry = call(
            state_kernel,
            [
                per_head,
                ((heads, tokens), f32),
                per_head,
                ((tokens, 1), f32),
                ((1, tokens), f32),
                ((ns, inner), bf16),
                ((1, inner), f32),
            ],
        )(pack, raw, raw_t, ids_c, ids_r, x, b_t)
        full, entering, carries = call(
            functools.partial(gather_kernel, n_dp, n_seq),
            [
                ((n, share, model), bf16),
                ((n_seq, piece, inner), bf16),
                ((n_seq, 1, inner), f32),
            ],
            [
                pltpu.VMEM((n_seq, piece, inner), bf16),
                pltpu.VMEM((n_seq, piece, inner), bf16),
                dma((n,)),
                dma((n,)),
            ]
            + [dma((n_seq,))] * 6,
            0,
        )(rows_b, state.reshape(n_seq, piece, inner), carry)
        weight = full.reshape(n * share, model)
        entering = entering.reshape(ns, inner)
        weight_grad, state_grad, row_dot, col_dot, small, loss = call(
            mix_kernel,
            [
                ((inner, model), bf16),
                ((ns, inner), bf16),
                per_head,
                per_head,
                ((8, inner), f32),
                ((1, 1), f32),
            ],
            [
                pltpu.VMEM((tokens, inner), bf16),
                pltpu.VMEM((tokens, inner), f32),
                pltpu.VMEM((tokens, inner), bf16),
                pltpu.VMEM((tokens, inner), f32),
            ],
        )(
            pack, sums, sums_t, width, seg_c, seg_r, x, z, b, c, b_t, c_t, target, weight,
            entering, scored, scale,
        )
        grad_rows, after = call(
            functools.partial(scatter_kernel, n_dp, n_seq),
            [((share, model), f32), ((n_seq, piece, inner), bf16)],
            [
                pltpu.VMEM((n, share, model), bf16),
                pltpu.VMEM((n_seq, piece, inner), bf16),
                pltpu.VMEM((n_seq, piece, inner), bf16),
                dma((n,)),
                dma((n,)),
            ]
            + [dma((n_seq,))] * 4,
            1,
        )(
            weight_grad.reshape(n, share, model),
            state_grad.reshape(n_seq, piece, inner),
            carries,
        )
        part = call(back_kernel, [((pack_rows, LANES), f32)])(
            pack, raw, sums, width, seg_c, x, b, after.reshape(ns, inner), entering, carry,
            row_dot, col_dot, small, loss, grad_rows,
        )[0]
        pack, rows, rows_b, loss_row = call(
            functools.partial(update_kernel, n_dp, n_seq, inner),
            [
                ((pack_rows, LANES), f32),
                ((share, model), f32),
                ((share, model), bf16),
                ((1, LANES), f32),
            ],
            [pltpu.VMEM((n, pack_rows, LANES), f32), dma((n,)), dma((n,))],
            2,
        )(part, pack, rows, grad_rows)
        losses.append(loss_row[0, 0] / total_count)
    return (
        jnp.stack(losses),
        rows,
        pack[g, :heads],
        pack[g + 1, :heads],
        pack[g + 2, :heads],
        pack[:g].reshape(inner),
    )


def solution(mesh):
    in_specs = (
        P("dp", "seq", None),
        P("dp", "seq", None),
        P("dp", "seq", None),
        P("dp", "seq", None),
        P("dp", "seq"),
        P(),
        P("dp", "seq", None),
        P(("dp", "seq"), None),
        P(),
        P(),
        P(),
        P(),
    )
    out_specs = (P(), P(("dp", "seq"), None), P(), P(), P(), P())
    return jax.shard_map(
        functools.partial(per_device, mesh.shape["dp"], mesh.shape["seq"]),
        mesh=mesh,
        in_specs=in_specs,
        out_specs=out_specs,
        check_vma=False,
    )
```

time: 1200 us -> 362 us (0.30); the launches traced: 1180 us -> 361 us
  Pallas kernels: 0 us -> 337 us
  blocking collectives: 292 us -> 0 us
  matrix products: 265 us -> 0 us
  local copies, waits for them, and re-layouts: 232 us -> 15.1 us
  loops' own time: 166 us -> 0 us
  other arithmetic: 131 us -> 6.11 us
  waiting for transfers between devices: 71.6 us -> 0 us
  between operations: 22.6 us -> 2.67 us
    pallas_call x0 -> x12, Pallas kernels: none -> 337 us  [run(): pl.pallas_call(body, out_shape=tuple((jax.ShapeDtypeStruct(*o) for o in o...]
    dot_general x111 -> x0, matrix products: 265 us -> none  [the longest x96 219 us: one_head(): return jnp.dot(decay_grid * scores, head_scaled, precision=highest)]
    all_gather x6 -> x0, blocking collectives: 217 us -> none  [the longest x2 130 us: joined(): gathered = jax.tree.map(lambda a: lax.all_gather(a, axis), part)]
    another operation x10 -> x0, loops' own time: 166 us -> none  [the longest x2 164 us: joined(): lax.fori_loop(1, lax.axis_size(axis), lambda source, state: combine(state...]
    dynamic_slice x290 -> x0, local copies, waits for them, and re-layouts: 146 us -> none  [the longest x258 134 us: take(): lax.dynamic_index_in_dim(a, source, 0, False)]
    unnamed x2 -> x0, blocking collectives: 74.3 us -> none
    reduce_scatter x2 -> x0, waiting for transfers between devices: 47.6 us -> none  [per_device(): lax.psum_scatter(weight_grad, ('dp', 'seq'), scatter_dimension=0, tiled=T...]
    dynamic_update_slice x32 -> x0, other arithmetic: 40.7 us -> none  [mix_block(): lax.map(one_head, (decay_sum.T, jnp.transpose(scaled, (1, 0, 2))))]
  transfers between devices with their start and end apart: 8 -> 0, of which waited for: 3 -> 0; matrix products, arithmetic and copies ran while one was open for 35% -> 0% of each run, Pallas kernels for 0% -> 0%
where the time goes in v1:
time: 362 us; the launch traced here: 361 us
  Pallas kernels  337 us (93%)
  local copies, waits for them, and re-layouts  15.1 us (4%)
  other arithmetic  6.11 us (2%)
    pallas_call x12, Pallas kernels, run(): pl.pallas_call(body, out_shape=tuple((jax.ShapeDtypeStruct(*o) for o in o...  337 us

profile of v1, /device:TPU:0, one launch (start us, length us, event | category | flops | bytes accessed | tf_op | source)
XLA Modules:
  0.0 361.1 jit_solution(8609200600710746800)
XLA Ops:
  0.6 1.3 reduce_sum.9
  2.6 1.2 dynamic_slice.4
  3.9 0.7 pad_bitcast_fusion.2
  4.5 0.7 pad_bitcast_fusion
  5.2 1.9 concatenate.3.pack
  7.1 1.5 convert_element_type.21.rows_b
  8.6 1.3 fusion.scale
  10.0 1.4 fusion.1.scored
  11.3 1.5 copy.25.ids_c
  12.8 1.1 copy.23
  13.9 0.7 fusion.2
  14.6 1.6 copy.22
  16.2 1.6 slice_bitcast_fusion
  17.8 3.7 %shard_map.163 = (f32[384,16]{1,0:T(8,128)}, f32[16,384]{1,0:T(8,128)}, f32[384,16]{1,0:T(8,128)}, f32[384,1]{1,0:T(8,128)}, f32[1,384]{1,0:T(1,128)}, /*index=5*/bf16[128,1024]{1,0:T(8,128)(2,1)}, f32[1,1024]{1,0:T(1,128)}) custom-call(f32[16,128]{1,0:T(8,128)} %concatenate.3.pack, f32[384,16]{1,0:T(8,128)} %bitcast.54, f32[16,384]{1,0:T(8,128)} %bitcast.77, ...), custom_call_target="tpu_custom_call" | custom-call | tf_op jit(solution)/shard_map/pallas_call | solution.py:416
  21.5 68.5 %shard_map.164 = (bf16[32,32,1024]{2,1,0:T(8,128)(2,1)}, bf16[8,16,1024]{2,1,0:T(8,128)(2,1)}, f32[8,1,1024]{2,1,0:T(1,128)}) custom-call(bf16[32,1024]{1,0:T(8,128)(2,1)} %convert_element_type.21.rows_b, bf16[8,16,1024]{2,1,0:T(8,128)(2,1)} %bitcast.76, f32[1,1024]{1,0:T(1,128)} %get-tuple-element.55.carry), custom_call_target="tpu_custom_call" | custom-call | tf_op jit(solution)/shard_map/pallas_call | solution.py:416
  90.0 13.2 %shard_map.165 = (bf16[1024,1024]{1,0:T(8,128)(2,1)}, bf16[128,1024]{1,0:T(8,128)(2,1)}, f32[384,16]{1,0:T(8,128)}, f32[384,16]{1,0:T(8,128)}, f32[8,1024]{1,0:T(8,128)}, /*index=5*/f32[1,1]{1,0:T(1,128)}) custom-call(f32[16,128]{1,0:T(8,128)} %concatenate.3.pack, f32[384,16]{1,0:T(8,128)} %get-tuple-element.49.sums, f32[16,384]{1,0:T(8,128)} %get-tuple-element.52.sums_t, ...), custom_call_target="tpu_custom_call" | custom-call | tf_op jit(solution)/shard_map/pallas_call | solution.py:416
  103.3 64.1 %shard_map.166 = (f32[32,1024]{1,0:T(8,128)}, bf16[8,16,1024]{2,1,0:T(8,128)(2,1)}) custom-call(bf16[32,32,1024]{2,1,0:T(8,128)(2,1)} %bitcast.63, bf16[8,16,1024]{2,1,0:T(8,128)(2,1)} %bitcast.74, f32[8,1,1024]{2,1,0:T(1,128)} %get-tuple-element.60.carries), custom_call_target="tpu_custom_call" | custom-call | tf_op jit(solution)/shard_map/pallas_call | solution.py:416
  167.4 5.2 %shard_map.167.part = f32[16,128]{1,0:T(8,128)} custom-call(f32[16,128]{1,0:T(8,128)} %concatenate.3.pack, f32[384,16]{1,0:T(8,128)} %bitcast.55, f32[384,16]{1,0:T(8,128)} %get-tuple-element.49.sums, f32[384,16]{1,0:T(8,128)} %get-tuple-element.50.width, f32[384,1]{1,0:T(8,128)} %get-tuple-element.51.seg_c, bf16[384,1024]{1,0:T(8,128)(2,1)} %bitcast.50, ...), custom_call_target="tpu_custom_call" | custom-call | tf_op jit(solution)/shard_map/pallas_call | solution.py:416
  172.6 15.3 %shard_map.168 = (f32[16,128]{1,0:T(8,128)}, f32[32,1024]{1,0:T(8,128)}, bf16[32,1024]{1,0:T(8,128)(2,1)}, f32[1,128]{1,0:T(1,128)}) custom-call(f32[16,128]{1,0:T(8,128)} %shard_map.167.part, f32[16,128]{1,0:T(8,128)} %concatenate.3.pack, f32[32,1024]{1,0:T(8,128)} %rows.1, f32[32,1024]{1,0:T(8,128)} %get-tuple-element.66.grad_rows), custom_call_target="tpu_custom_call" | custom-call | tf_op jit(solution)/shard_map/pallas_call | solution.py:416
  188.5 3.7 %shard_map.169 = (f32[384,16]{1,0:T(8,128)}, f32[16,384]{1,0:T(8,128)}, f32[384,16]{1,0:T(8,128)}, f32[384,1]{1,0:T(8,128)}, f32[1,384]{1,0:T(1,128)}, /*index=5*/bf16[128,1024]{1,0:T(8,128)(2,1)}, f32[1,1024]{1,0:T(1,128)}) custom-call(f32[16,128]{1,0:T(8,128)} %get-tuple-element.68.pack, f32[384,16]{1,0:T(8,128)} %bitcast.56, f32[16,384]{1,0:T(8,128)} %bitcast.78, ...), custom_call_target="tpu_custom_call" | custom-call | tf_op jit(solution)/shard_map/pallas_call | solution.py:416
  192.3 65.5 %shard_map.170 = (bf16[32,32,1024]{2,1,0:T(8,128)(2,1)}, bf16[8,16,1024]{2,1,0:T(8,128)(2,1)}, f32[8,1,1024]{2,1,0:T(1,128)}) custom-call(bf16[32,1024]{1,0:T(8,128)(2,1)} %get-tuple-element.74.rows_b, bf16[8,16,1024]{2,1,0:T(8,128)(2,1)} %bitcast.75, f32[1,1024]{1,0:T(1,128)} %get-tuple-element.76.carry), custom_call_target="tpu_custom_call" | custom-call | tf_op jit(solution)/shard_map/pallas_call | solution.py:416
  257.7 13.2 %shard_map.171 = (bf16[1024,1024]{1,0:T(8,128)(2,1)}, bf16[128,1024]{1,0:T(8,128)(2,1)}, f32[384,16]{1,0:T(8,128)}, f32[384,16]{1,0:T(8,128)}, f32[8,1024]{1,0:T(8,128)}, /*index=5*/f32[1,1]{1,0:T(1,128)}) custom-call(f32[16,128]{1,0:T(8,128)} %get-tuple-element.68.pack, f32[384,16]{1,0:T(8,128)} %get-tuple-element.69.sums, ...), custom_call_target="tpu_custom_call" | custom-call | tf_op jit(solution)/shard_map/pallas_call | solution.py:416
  271.0 64.5 %shard_map.172 = (f32[32,1024]{1,0:T(8,128)}, bf16[8,16,1024]{2,1,0:T(8,128)(2,1)}) custom-call(bf16[32,32,1024]{2,1,0:T(8,128)(2,1)} %bitcast.62, bf16[8,16,1024]{2,1,0:T(8,128)(2,1)} %bitcast.71, f32[8,1,1024]{2,1,0:T(1,128)} %get-tuple-element.81.carries), custom_call_target="tpu_custom_call" | custom-call | tf_op jit(solution)/shard_map/pallas_call | solution.py:416
  335.5 5.2 %shard_map.173.part = f32[16,128]{1,0:T(8,128)} custom-call(f32[16,128]{1,0:T(8,128)} %get-tuple-element.68.pack, f32[384,16]{1,0:T(8,128)} %bitcast.57, f32[384,16]{1,0:T(8,128)} %get-tuple-element.69.sums, f32[384,16]{1,0:T(8,128)} %get-tuple-element.70.width, f32[384,1]{1,0:T(8,128)} %get-tuple-element.71.seg_c, bf16[384,1024]{1,0:T(8,128)(2,1)} %bitcast.53, ...), custom_call_target="tpu_custom_call" | custom-call | tf_op jit(solution)/shard_map/pallas_call | solution.py:416
  340.7 15.0 %shard_map.174 = (f32[16,128]{1,0:T(8,128)}, f32[32,1024]{1,0:T(8,128)}, bf16[32,1024]{1,0:T(8,128)(2,1)}, f32[1,128]{1,0:T(1,128)}) custom-call(f32[16,128]{1,0:T(8,128)} %shard_map.173.part, f32[16,128]{1,0:T(8,128)} %get-tuple-element.68.pack, f32[32,1024]{1,0:T(8,128)} %get-tuple-element.88.rows, f32[32,1024]{1,0:T(8,128)} %get-tuple-element.87.grad_rows), custom_call_target="tpu_custom_call" | custom-call | tf_op jit(solution)/shard_map/pallas_call | solution.py:416
  356.4 0.6 pad_maximum_fusion
  356.9 1.3 slice_bitcast_fusion.3
  358.3 1.3 slice_bitcast_fusion.2
  359.5 1.6 copy.30
  (1 shorter events, 0.0 us)

commit v2 on v1

v2 whole, which is shorter than its diff:
```python
import functools

import jax
import jax.numpy as jnp
from jax import lax
from jax.experimental import pallas as pl
from jax.experimental.pallas import tpu as pltpu
from jax.sharding import PartitionSpec as P

STEPS = 2
norm_floor = 1.0
clip_limit = 1.0
learn_rate = 8.0
highest = lax.Precision.HIGHEST
f32 = jnp.float32
bf16 = jnp.bfloat16
LANES = 128
VMEM = pl.BlockSpec(memory_space=pltpu.VMEM)
SMEM = pl.BlockSpec(memory_space=pltpu.SMEM)
MESH = pl.DeviceIdType.MESH
LIMIT = 60 * 1024 * 1024


def dot(a, b, **kw):
    return jnp.dot(a, b, preferred_element_type=f32, **kw)


def spread_matrix(heads, width):
    size = width // heads
    lane = lax.broadcasted_iota(jnp.int32, (heads, width), 1)
    head = lax.broadcasted_iota(jnp.int32, (heads, width), 0)
    return ((lane >= head * size) & (lane < (head + 1) * size)).astype(bf16)


def split(a):
    high = a.astype(bf16)
    return high, (a - high.astype(f32)).astype(bf16)


def spread(a, ones):
    high, low = split(a)
    return dot(high, ones) + dot(low, ones)


def head_sum(a, ones):
    high, low = split(a)
    turn = (((1,), (1,)), ((), ()))
    one = functools.partial(
        lax.dot_general, dimension_numbers=turn, preferred_element_type=f32
    )
    return one(high, ones) + one(low, ones)


def column(row):
    n = row.shape[1]
    i = lax.broadcasted_iota(jnp.int32, (n, n), 0)
    j = lax.broadcasted_iota(jnp.int32, (n, n), 1)
    return jnp.sum(jnp.where(i == j, row, 0.0), axis=1, keepdims=True)


def gain_rows(width):
    return width // LANES


def state_kernel(
    pack, raw, raw_t, ids_r, x, proj, rows, sums, sums_t, width, seg_c, seg_r, state, carry, rows_b
):
    tokens, heads = raw.shape
    inner = x.shape[1]
    g = gain_rows(inner)
    ones = spread_matrix(heads, inner)
    rate_row = -jnp.exp(pack[g : g + 1, :heads])
    bias_row = pack[g + 1 : g + 2, :heads]
    w = jax.nn.softplus(raw[...] + bias_row)
    w_t = jax.nn.softplus(raw_t[...] + column(bias_row))
    i = lax.broadcasted_iota(jnp.int32, (tokens, tokens), 0)
    j = lax.broadcasted_iota(jnp.int32, (tokens, tokens), 1)
    lower = (i >= j).astype(f32)
    upper = (i <= j).astype(f32)
    s = dot(lower, w * rate_row, precision=highest)
    sums[...] = s
    sums_t[...] = dot(w_t * column(rate_row), upper, precision=highest)
    width[...] = w
    stop = jnp.where(ids_r[...] == 0, 1.0, 0.0)
    sc = jnp.sum(jnp.where(i >= j, stop, 0.0), axis=1, keepdims=True)
    sr = jnp.sum(jnp.where(i <= j, column(stop), 0.0), axis=0, keepdims=True)
    rows_b[...] = rows[...].astype(bf16)
    seg_c[...] = sc
    seg_r[...] = sr
    last = sc[tokens - 1 : tokens, :]
    final = s[tokens - 1 : tokens, :]
    tail = jnp.where(sc == last, jnp.exp(final - s), 0.0)
    weighted = (x[...].astype(f32) * spread(w * tail, ones)).astype(bf16)
    b = proj[:, : proj.shape[1] // 2]
    state[...] = lax.dot_general(
        b, weighted, (((0,), (0,)), ((), ())), preferred_element_type=f32
    ).astype(bf16)
    kept = jnp.where(last == 0.0, jnp.exp(final), 0.0)
    carry[...] = spread(jnp.broadcast_to(kept, (8, heads)), ones)[0:1, :]


def mix_kernel(
    n_dp, counts, pack, sums, sums_t, width, seg_c, seg_r, x, z, proj, target, weight, state,
    weight_grad, state_grad, row_dot, col_dot, small, loss,
    scaled, mixed, slope_b, prod,
):
    tokens, heads = sums.shape
    inner = x.shape[1]
    g = gain_rows(inner)
    per = LANES // (inner // heads)
    size = inner // heads
    ones = spread_matrix(heads, inner)
    s = sums[...]
    xf = x[...].astype(f32)
    scaled[...] = (xf * spread(width[...], ones)).astype(bf16)
    i = lax.broadcasted_iota(jnp.int32, (tokens, tokens), 0)
    j = lax.broadcasted_iota(jnp.int32, (tokens, tokens), 1)
    same = seg_c[...] == seg_r[...]
    ns = proj.shape[1] // 2
    b, c = proj[:, :ns], proj[:, ns:]
    turn = functools.partial(lax.dot_general, preferred_element_type=f32)
    scores = jnp.where(same & (i >= j), turn(c, b, (((1,), (1,)), ((), ()))), 0.0)
    entry = spread(jnp.where(seg_c[...] == 0.0, jnp.exp(s), 0.0), ones)
    mixed[...] = dot(c, state[...]) * entry
    lane = lax.broadcasted_iota(jnp.int32, (LANES, LANES), 1)
    for k in range(inner // LANES):
        cols = slice(k * LANES, (k + 1) * LANES)
        for at in range(0, tokens, LANES):
            rows = slice(at, at + LANES)
            end = at + LANES
            total = None
            for p in range(per):
                h = k * per + p
                gap = sums[rows, h : h + 1] - sums_t[h : h + 1, :end]
                grid = (jnp.exp(jnp.minimum(gap, 0.0)) * scores[rows, :end]).astype(bf16)
                part = dot(grid, scaled[:end, cols])
                total = part if total is None else jnp.where(lane < p * size, total, part)
            mixed[rows, cols] += total
    gain = jnp.concatenate([pack[k : k + 1, :] for k in range(g)], axis=1)
    skip = spread(jnp.broadcast_to(pack[g + 2 : g + 3, :heads], (8, heads)), ones)[0:1, :]
    zf = z[...].astype(f32)
    silu = zf * jax.nn.sigmoid(zf)
    gated = (mixed[...] + skip * xf) * silu
    root = lax.rsqrt(jnp.mean(gated * gated, axis=1, keepdims=True) + norm_floor)
    normed = (gated * gain * root).astype(bf16)
    residual = dot(normed, weight[...]) - target[...].astype(f32)
    model = target.shape[1]
    total_count = counts[0]
    for k in range(1, n_dp):
        total_count = total_count + counts[k]
    share = 1.0 / (model * total_count.astype(f32))
    position = lax.axis_index("seq") * tokens + lax.broadcasted_iota(jnp.int32, (tokens, 1), 0)
    scored = jnp.where(position < counts[lax.axis_index("dp")], 1.0, 0.0)
    token_loss = jnp.sum(residual * residual, axis=1, keepdims=True) * scored
    loss[...] = jnp.sum(token_loss, axis=0, keepdims=True) * share
    out_grad = (residual * (2.0 * share * scored)).astype(bf16)
    weight_grad[...] = lax.dot_general(
        normed, out_grad, (((0,), (0,)), ((), ())), preferred_element_type=f32
    ).astype(bf16)
    normed_grad = lax.dot_general(
        out_grad, weight[...], (((1,), (1,)), ((), ())), preferred_element_type=f32
    )
    lifted = normed_grad * gated
    gain_grad = jnp.sum(lifted * root, axis=0, keepdims=True)
    inward = jnp.sum(lifted * gain, axis=1, keepdims=True) * (root * root * root / inner)
    dy = (normed_grad * gain * root - gated * inward) * silu
    small[0:1, :] = gain_grad
    small[1:2, :] = jnp.sum(dy * xf, axis=0, keepdims=True)
    row_dot[...] = head_sum(dy * mixed[...], ones)
    state_grad[...] = turn(c, (entry * dy).astype(bf16), (((0,), (0,)), ((), ()))).astype(bf16)
    slope_b[...] = dy.astype(bf16)
    scores_t = turn(b, c, (((1,), (1,)), ((), ())))
    same_t = (seg_c[...] == seg_r[...]) & (i <= j)
    scores_t = jnp.where(same_t, scores_t, 0.0)
    for k in range(inner // LANES):
        cols = slice(k * LANES, (k + 1) * LANES)
        for at in range(0, tokens, LANES):
            rows = slice(at, at + LANES)
            total = None
            for p in range(per):
                h = k * per + p
                gap = sums_t[h : h + 1, at:] - sums[rows, h : h + 1]
                grid = (jnp.exp(jnp.minimum(gap, 0.0)) * scores_t[rows, at:]).astype(bf16)
                part = dot(grid, slope_b[at:, cols])
                total = part if total is None else jnp.where(lane < p * size, total, part)
            prod[rows, cols] = total * x[rows, cols].astype(f32)
    col_dot[...] = head_sum(prod[...], ones)


def back_kernel(
    pack, raw, sums, width, seg_c, x, proj, after, state, carry, row_dot, col_dot, small, loss,
    grad_rows, out,
):
    tokens, heads = sums.shape
    inner = x.shape[1]
    g = gain_rows(inner)
    ones = spread_matrix(heads, inner)
    s = sums[...]
    w = width[...]
    rate_row = -jnp.exp(pack[g : g + 1, :heads])
    bias_row = pack[g + 1 : g + 2, :heads]
    sc = seg_c[...]
    last = sc[tokens - 1 : tokens, :]
    final = s[tokens - 1 : tokens, :]
    tail = jnp.where(sc == last, jnp.exp(final - s), 0.0)
    pulled = head_sum(dot(proj[:, : proj.shape[1] // 2], after[...]) * x[...].astype(f32), ones) * tail
    moved = after[...].astype(f32) * state[...].astype(f32)
    both = jnp.concatenate(
        [
            jnp.sum(moved, axis=0, keepdims=True) * carry[...],
            small[1:2, :],
            jnp.zeros((6, inner), f32),
        ],
        axis=0,
    )
    both = head_sum(both, ones)
    col = col_dot[...] + pulled
    d_sums = row_dot[...] - w * col
    d_final = jnp.sum(w * pulled, axis=0, keepdims=True) + both[0:1, :]
    i = lax.broadcasted_iota(jnp.int32, (tokens, tokens), 0)
    j = lax.broadcasted_iota(jnp.int32, (tokens, tokens), 1)
    d_rate = dot((i <= j).astype(f32), d_sums, precision=highest) + d_final
    d_width = (col + rate_row * d_rate) * jax.nn.sigmoid(raw[...] + bias_row)
    rows = grad_rows[...]
    square = jnp.sum(jnp.sum(rows * rows, axis=1, keepdims=True), axis=0, keepdims=True)
    out[...] = jnp.zeros(out.shape, f32)
    for k in range(g):
        out[k : k + 1, :] = small[0:1, k * LANES : (k + 1) * LANES]
    out[g : g + 1, :heads] = rate_row * jnp.sum(d_rate * w, axis=0, keepdims=True)
    out[g + 1 : g + 2, :heads] = jnp.sum(d_width, axis=0, keepdims=True)
    out[g + 2 : g + 3, :heads] = both[1:2, :]
    out[g + 3 : g + 4, :] = jnp.broadcast_to(loss[...], (1, LANES))
    out[g + 4 : g + 5, :] = jnp.broadcast_to(square, (1, LANES))


class Spot:
    def __init__(self, n_dp, n_seq):
        self.n_dp, self.n_seq = n_dp, n_seq
        self.cores = 2 if n_dp % 2 == 0 else 1
        self.ys = n_dp // self.cores
        self.highs = 4 if n_seq % 4 == 0 else n_seq
        self.lows = n_seq // self.highs
        self.dp, self.seq = lax.axis_index("dp"), lax.axis_index("seq")
        self.y, self.core = self.dp // self.cores, self.dp % self.cores
        self.high, self.low = self.seq // self.lows, self.seq % self.lows
        self.me = self.dp * n_seq + self.seq

    def core_peer(self, t):
        return (self.y * self.cores + (self.core + t) % self.cores, self.seq)

    def y_peer(self, t):
        return (((self.y + t) % self.ys) * self.cores + self.core, self.seq)

    def low_peer(self, t):
        return (self.dp, self.high * self.lows + (self.low + t) % self.lows)

    def high_peer(self, t):
        return (self.dp, ((self.high + t) % self.highs) * self.lows + self.low)

    def seq_peer(self, t):
        return (self.dp, (self.seq + t) % self.n_seq)

    def meet(self, with_seq):
        barrier = pltpu.get_barrier_semaphore()
        groups = [(self.cores, self.core_peer), (self.ys, self.y_peer)]
        if with_seq:
            groups.append((self.n_seq, self.seq_peer))
        else:
            groups += [(self.lows, self.low_peer), (self.highs, self.high_peer)]
        for count, peer in groups:
            each(
                count,
                lambda t, peer=peer: pl.semaphore_signal(
                    barrier, inc=1, device_id=peer(t), device_id_type=MESH
                ),
            )
        pl.semaphore_wait(barrier, sum(count - 1 for count, _ in groups))


def each(n, body, first=1):
    def one(t, _):
        body(t)
        return 0

    lax.fori_loop(first, n, one, 0)


def remote(source, target, send, recv, peer):
    return pltpu.make_async_remote_copy(
        src_ref=source,
        dst_ref=target,
        send_sem=send,
        recv_sem=recv,
        device_id=peer,
        device_id_type=MESH,
    )


def gather_kernel(
    n_dp, n_seq, rows_b, state, carry, full, entering, carries,
    landed, ready, own_sem, w_recv, high_send, low_send, y_send, core_send,
    s_send, s_recv, c_send, c_recv, r_send, r_recv,
):
    at = Spot(n_dp, n_seq)
    own = pltpu.make_async_copy(rows_b, full.at[at.me], own_sem)
    own.start()
    at.meet(True)
    mine = at.seq
    back = lambda t: (mine + n_seq - t) % n_seq

    def lead(t):
        return remote(carry, carries.at[mine], c_send.at[t], c_recv.at[t], at.seq_peer(t))

    def lead_in(t):
        return remote(carry, carries.at[back(t)], c_send.at[t], c_recv.at[t], at.seq_peer(t))

    def first(t):
        p = (mine + t) % n_seq
        return remote(state.at[p], landed.at[mine], s_send.at[t], s_recv.at[t], at.seq_peer(t))

    def first_in(t):
        p = back(t)
        return remote(state.at[p], landed.at[p], s_send.at[t], s_recv.at[t], at.seq_peer(t))

    def second(t):
        p = (mine + t) % n_seq
        return remote(ready.at[p], entering.at[mine], r_send.at[t], r_recv.at[t], at.seq_peer(t))

    def second_in(t):
        p = back(t)
        return remote(ready.at[p], entering.at[p], r_send.at[t], r_recv.at[t], at.seq_peer(t))

    def push(chunk, send, peer):
        return remote(full.at[chunk], full.at[chunk], send, w_recv.at[chunk], peer)

    def high_edge(t):
        return push(at.me, high_send.at[t], at.high_peer(t))

    def low_edge(t, high):
        chunk = at.dp * n_seq + high * at.lows + at.low
        return push(chunk, low_send.at[t * at.highs + high], at.low_peer(t))

    def y_edge(t, seq):
        return push(at.dp * n_seq + seq, y_send.at[t * n_seq + seq], at.y_peer(t))

    def core_edge(t, y, seq):
        chunk = (y * at.cores + at.core) * n_seq + seq
        return push(chunk, core_send.at[(t * at.ys + y) * n_seq + seq], at.core_peer(t))

    def arrived(chunk):
        push(chunk, high_send.at[0], at.core_peer(1)).wait_recv()

    def onward(y, seq, to_low, to_y):
        if to_low:
            each(at.lows, lambda t: low_edge(t, seq // at.lows).start())
        if to_y:
            each(at.ys, lambda t: y_edge(t, seq).start())
        each(at.cores, lambda t: core_edge(t, y, seq).start())

    def start(t):
        lead(t).start()
        first(t).start()

    each(n_seq, start)
    own.wait()
    each(at.highs, lambda t: high_edge(t).start())
    onward(at.y, at.seq, True, True)
    carries[mine] = carry[...]
    landed[mine] = state[mine]

    def from_high(t):
        seq = ((at.high + at.highs - t) % at.highs) * at.lows + at.low
        arrived(at.dp * n_seq + seq)
        onward(at.y, seq, True, True)

    each(at.highs, from_high)

    def from_low(t):
        low = (at.low + at.lows - t) % at.lows

        def one(u):
            seq = ((at.high + at.highs - u) % at.highs) * at.lows + low
            arrived(at.dp * n_seq + seq)
            onward(at.y, seq, False, True)

        each(at.highs, one, 0)

    each(at.lows, from_low)

    def arrive(t):
        lead_in(t).wait_recv()
        first_in(t).wait_recv()

    each(n_seq, arrive)
    running = jnp.zeros(state.shape[1:], f32)
    for d in range(n_seq):
        ready[d] = running.astype(bf16)
        if d < n_seq - 1:
            running = carries[d] * running + landed[d].astype(f32)
    each(n_seq, lambda t: second(t).start())
    entering[mine] = ready[mine]

    def from_y(t):
        y = (at.y + at.ys - t) % at.ys

        def one(u):
            high, low = u % at.highs, u // at.highs
            seq = ((at.high + high) % at.highs) * at.lows + (at.low + low) % at.lows
            arrived((y * at.cores + at.core) * n_seq + seq)
            onward(y, seq, False, False)

        each(n_seq, one, 0)

    each(at.ys, from_y)
    each(n_seq, lambda t: second_in(t).wait_recv())

    def from_core(t):
        core = (at.core + t) % at.cores

        def one(k):
            arrived(((k // n_seq) * at.cores + core) * n_seq + k % n_seq)

        each(at.ys * n_seq, one, 0)

    each(at.cores, from_core)

    def sent(t):
        lead(t).wait_send()
        first(t).wait_send()
        second(t).wait_send()

    each(n_seq, sent)
    each(at.highs, lambda t: high_edge(t).wait_send())
    each(at.lows, lambda t: each(at.highs, lambda k: low_edge(t, k).wait_send(), 0))
    each(at.ys, lambda t: each(n_seq, lambda k: y_edge(t, k).wait_send(), 0))
    each(
        at.cores,
        lambda t: each(
            at.ys * n_seq, lambda k: core_edge(t, k // n_seq, k % n_seq).wait_send(), 0
        ),
    )


def scatter_kernel(
    n_dp, n_seq, grad, state, carries, total, leaving,
    staged, from_core, from_y, from_low, from_high, landed, ready,
    core_send, core_recv, y_send, y_recv, low_send, low_recv, high_send, high_recv,
    s_send, s_recv, r_send, r_recv,
):
    at = Spot(n_dp, n_seq)
    at.meet(True)
    mine = at.seq
    back = lambda t: (mine + n_seq - t) % n_seq

    def first(t):
        p = (mine + t) % n_seq
        return remote(state.at[p], landed.at[mine], s_send.at[t], s_recv.at[t], at.seq_peer(t))

    def first_in(t):
        p = back(t)
        return remote(state.at[p], landed.at[p], s_send.at[t], s_recv.at[t], at.seq_peer(t))

    def second(t):
        p = (mine + t) % n_seq
        return remote(ready.at[p], leaving.at[mine], r_send.at[t], r_recv.at[t], at.seq_peer(t))

    def second_in(t):
        p = back(t)
        return remote(ready.at[p], leaving.at[p], r_send.at[t], r_recv.at[t], at.seq_peer(t))

    def core_edge(t, y, seq):
        core = (at.core + t) % at.cores
        k = (t * at.ys + y) * n_seq + seq
        return remote(
            grad.at[(y * at.cores + core) * n_seq + seq], from_core.at[k],
            core_send.at[k], core_recv.at[k], at.core_peer(t),
        )

    def y_edge(t, seq):
        k = t * n_seq + seq
        y = (at.y + t) % at.ys
        return remote(
            staged.at[y * n_seq + seq], from_y.at[k], y_send.at[k], y_recv.at[k], at.y_peer(t)
        )

    def low_edge(t, high):
        k = t * at.highs + high
        seq = high * at.lows + (at.low + t) % at.lows
        return remote(
            staged.at[at.y * n_seq + seq], from_low.at[k],
            low_send.at[k], low_recv.at[k], at.low_peer(t),
        )

    def high_edge(t):
        seq = ((at.high + t) % at.highs) * at.lows + at.low
        return remote(
            staged.at[at.y * n_seq + seq], from_high.at[t],
            high_send.at[t], high_recv.at[t], at.high_peer(t),
        )

    def chip_sum(y, seq):
        acc = grad[(y * at.cores + at.core) * n_seq + seq].astype(f32)
        for t in range(1, at.cores):
            core_edge(t, y, seq).wait_recv()
            acc = acc + from_core[(t * at.ys + y) * n_seq + seq].astype(f32)
        return acc

    def y_sum(seq):
        acc = chip_sum(at.y, seq)
        for t in range(1, at.ys):
            y_edge(t, seq).wait_recv()
            acc = acc + from_y[t * n_seq + seq].astype(f32)
        return acc

    def low_sum(high):
        acc = y_sum(high * at.lows + at.low)
        for t in range(1, at.lows):
            low_edge(t, high).wait_recv()
            acc = acc + from_low[t * at.highs + high].astype(f32)
        return acc

    def order(u):
        low = (at.low + 1 + u // at.highs) % at.lows
        return ((at.high + 1 + u) % at.highs) * at.lows + low

    each(n_seq, lambda t: first(t).start())

    def to_core(t):
        def one(k):
            core_edge(t, (at.y + 1 + k // n_seq) % at.ys, order(k % n_seq)).start()

        each(at.ys * n_seq, one, 0)

    each(at.cores, to_core)
    landed[mine] = state[mine]

    def to_y(t):
        y = (at.y + t) % at.ys

        def one(u):
            seq = order(u)
            staged[y * n_seq + seq] = chip_sum(y, seq).astype(bf16)
            y_edge(t, seq).start()

        each(n_seq, one, 0)

    each(at.ys, to_y)
    each(n_seq, lambda t: first_in(t).wait_recv())
    running = jnp.zeros(state.shape[1:], f32)
    for d in reversed(range(n_seq)):
        ready[d] = running.astype(bf16)
        if d > 0:
            running = carries[d] * running + landed[d].astype(f32)
    each(n_seq, lambda t: second(t).start())
    leaving[mine] = ready[mine]

    def to_low(t):
        def one(u):
            high = (at.high + 1 + u) % at.highs
            seq = high * at.lows + (at.low + t) % at.lows
            staged[at.y * n_seq + seq] = y_sum(seq).astype(bf16)
            low_edge(t, high).start()

        each(at.highs, one, 0)

    each(at.lows, to_low)

    def to_high(t):
        high = (at.high + t) % at.highs
        staged[at.y * n_seq + high * at.lows + at.low] = low_sum(high).astype(bf16)
        high_edge(t).start()

    each(at.highs, to_high)
    acc = low_sum(at.high)
    for t in range(1, at.highs):
        high_edge(t).wait_recv()
        acc = acc + from_high[t].astype(f32)
    total[...] = acc
    each(n_seq, lambda t: second_in(t).wait_recv())

    def sent(t):
        first(t).wait_send()
        second(t).wait_send()

    each(n_seq, sent)
    each(at.highs, lambda t: high_edge(t).wait_send())
    each(at.lows, lambda t: each(at.highs, lambda k: low_edge(t, k).wait_send(), 0))
    each(at.ys, lambda t: each(n_seq, lambda k: y_edge(t, k).wait_send(), 0))
    each(
        at.cores,
        lambda t: each(
            at.ys * n_seq, lambda k: core_edge(t, k // n_seq, k % n_seq).wait_send(), 0
        ),
    )


def update_kernel(
    n_dp, n_seq, inner, part, pack, rows, grad_rows, new_pack, new_rows, loss,
    by_core, by_y, by_low, by_high, send, recv,
):
    at = Spot(n_dp, n_seq)
    at.meet(False)
    summed = part[...]
    levels = [
        (by_core, at.cores, at.core, at.core_peer),
        (by_y, at.ys, at.y, at.y_peer),
        (by_low, at.lows, at.low, at.low_peer),
        (by_high, at.highs, at.high, at.high_peer),
    ]
    base = 0
    for held, count, digit, peer in levels:
        held[digit] = summed

        def edge(t, slot, held=held, digit=digit, peer=peer, base=base):
            return remote(held.at[digit], held.at[slot], send.at[base + t], recv.at[base + t], peer(t))

        each(count, lambda t: edge(t, digit).start())
        each(count, lambda t: edge(t, (digit + count - t) % count).wait_recv())
        summed = held[0]
        for k in range(1, count):
            summed = summed + held[k]
        each(count, lambda t: edge(t, digit).wait_send())
        base += count
    g = gain_rows(inner)
    row = lax.broadcasted_iota(jnp.int32, summed.shape, 0)
    grads = jnp.where(row < g + 3, summed, 0.0)
    lane_sum = jnp.sum(grads * grads, axis=0, keepdims=True)
    norm_square = jnp.sum(lane_sum, axis=1, keepdims=True) + summed[g + 4 : g + 5, 0:1]
    factor = clip_limit / jnp.maximum(jnp.sqrt(norm_square), clip_limit)
    new_pack[...] = pack[...] - learn_rate * factor * grads
    new_rows[...] = rows[...] - learn_rate * factor * grad_rows[...]
    loss[...] = summed[g + 3 : g + 4, :]


def call(body, outs, scratch=(), collective=None):
    extra = {}
    if collective is not None:
        extra = {"collective_id": collective, "has_side_effects": True}

    def run(*args):
        return pl.pallas_call(
            body,
            out_shape=tuple(jax.ShapeDtypeStruct(*o) for o in outs),
            in_specs=[SMEM if a.ndim == 1 else VMEM for a in args],
            out_specs=tuple([VMEM] * len(outs)),
            scratch_shapes=list(scratch),
            compiler_params=pltpu.CompilerParams(vmem_limit_bytes=LIMIT, **extra),
        )(*args)

    return run


def per_device(
    n_dp,
    n_seq,
    head_inputs,
    gate_inputs,
    state_proj,
    time_steps,
    token_ids,
    token_counts,
    teacher_out,
    out_weight,
    decay_log,
    step_bias,
    skip_gain,
    norm_gain,
):
    n = n_dp * n_seq
    x, z, target, raw = head_inputs[0], gate_inputs[0], teacher_out[0], time_steps[0]
    tokens, inner = x.shape
    ns = state_proj.shape[2] // 2
    heads = decay_log.shape[0]
    model = target.shape[1]
    share = out_weight.shape[0]
    piece = ns // n_seq
    g = gain_rows(inner)
    pack_rows = -(-(g + 5) // 8) * 8
    proj = state_proj[0]
    raw_t = raw.T
    ids_r = token_ids
    wide = lambda a: jnp.pad(a, (0, LANES - heads))[None]
    pack = jnp.concatenate(
        [
            norm_gain.reshape(g, LANES),
            wide(decay_log),
            wide(step_bias),
            wide(skip_gain),
            jnp.zeros((pack_rows - g - 3, LANES), f32),
        ]
    )
    rows = out_weight
    dma = pltpu.SemaphoreType.DMA
    losses = []
    per_head = ((tokens, heads), f32)
    for _ in range(STEPS):
        sums, sums_t, width, seg_c, seg_r, state, carry, rows_b = call(
            state_kernel,
            [
                per_head,
                ((heads, tokens), f32),
                per_head,
                ((tokens, 1), f32),
                ((1, tokens), f32),
                ((ns, inner), bf16),
                ((1, inner), f32),
                ((share, model), bf16),
            ],
        )(pack, raw, raw_t, ids_r, x, proj, rows)
        full, entering, carries = call(
            functools.partial(gather_kernel, n_dp, n_seq),
            [
                ((n, share, model), bf16),
                ((n_seq, piece, inner), bf16),
                ((n_seq, 1, inner), f32),
            ],
            [
                pltpu.VMEM((n_seq, piece, inner), bf16),
                pltpu.VMEM((n_seq, piece, inner), bf16),
                dma,
                dma((n,)),
                dma((n_seq,)),
                dma((n_seq * n_seq,)),
                dma((n,)),
                dma((n,)),
            ]
            + [dma((n_seq,))] * 6,
            0,
        )(rows_b, state.reshape(n_seq, piece, inner), carry)
        weight = full.reshape(n * share, model)
        entering = entering.reshape(ns, inner)
        weight_grad, state_grad, row_dot, col_dot, small, loss = call(
            functools.partial(mix_kernel, n_dp),
            [
                ((inner, model), bf16),
                ((ns, inner), bf16),
                per_head,
                per_head,
                ((8, inner), f32),
                ((1, 1), f32),
            ],
            [
                pltpu.VMEM((tokens, inner), bf16),
                pltpu.VMEM((tokens, inner), f32),
                pltpu.VMEM((tokens, inner), bf16),
                pltpu.VMEM((tokens, inner), f32),
            ],
        )(
            token_counts, pack, sums, sums_t, width, seg_c, seg_r, x, z, proj, target, weight,
            entering,
        )
        grad_rows, after = call(
            functools.partial(scatter_kernel, n_dp, n_seq),
            [((share, model), f32), ((n_seq, piece, inner), bf16)],
            [
                pltpu.VMEM((n, share, model), bf16),
                pltpu.VMEM((n, share, model), bf16),
                pltpu.VMEM((n, share, model), bf16),
                pltpu.VMEM((n_seq, share, model), bf16),
                pltpu.VMEM((n_seq, share, model), bf16),
                pltpu.VMEM((n_seq, piece, inner), bf16),
                pltpu.VMEM((n_seq, piece, inner), bf16),
            ]
            + [dma((n,))] * 4
            + [dma((n_seq,))] * 8,
            1,
        )(
            weight_grad.reshape(n, share, model),
            state_grad.reshape(n_seq, piece, inner),
            carries,
        )
        part = call(back_kernel, [((pack_rows, LANES), f32)])(
            pack, raw, sums, width, seg_c, x, proj, after.reshape(ns, inner), entering, carry,
            row_dot, col_dot, small, loss, grad_rows,
        )[0]
        pack, rows, loss_row = call(
            functools.partial(update_kernel, n_dp, n_seq, inner),
            [
                ((pack_rows, LANES), f32),
                ((share, model), f32),
                ((1, LANES), f32),
            ],
            [pltpu.VMEM((k, pack_rows, LANES), f32) for k in (n_dp, n_dp, n_seq, n_seq)]
            + [dma((n,))] * 2,
            2,
        )(part, pack, rows, grad_rows)
        losses.append(loss_row[0, 0])
    return (
        jnp.stack(losses),
        rows,
        pack[g, :heads],
        pack[g + 1, :heads],
        pack[g + 2, :heads],
        pack[:g].reshape(inner),
    )


def solution(mesh):
    in_specs = (
        P("dp", "seq", None),
        P("dp", "seq", None),
        P("dp", "seq", None),
        P("dp", "seq", None),
        P("dp", "seq"),
        P(),
        P("dp", "seq", None),
        P(("dp", "seq"), None),
        P(),
        P(),
        P(),
        P(),
    )
    out_specs = (P(), P(("dp", "seq"), None), P(), P(), P(), P())
    return jax.shard_map(
        functools.partial(per_device, mesh.shape["dp"], mesh.shape["seq"]),
        mesh=mesh,
        in_specs=in_specs,
        out_specs=out_specs,
        check_vma=False,
    )
```

time: 362 us -> 201 us (0.56)
  Pallas kernels: 337 us -> 190 us
  local copies, waits for them, and re-layouts: 15.1 us -> 8.93 us
  other arithmetic: 6.11 us -> 1.22 us
    pallas_call x12, Pallas kernels: 337 us -> 190 us  [run(): pl.pallas_call(body, out_shape=tuple((jax.ShapeDtypeStruct(*o) for o in o...]
where the time goes in v2:
time: 201 us
  Pallas kernels  190 us (95%)
  local copies, waits for them, and re-layouts  8.93 us (4%)
    pallas_call x12, Pallas kernels, run(): pl.pallas_call(body, out_shape=tuple((jax.ShapeDtypeStruct(*o) for o in o...  190 us

profile of v2, /device:TPU:0, one launch (start us, length us, event | category | flops | bytes accessed | tf_op | source)
XLA Modules:
  0.0 200.6 jit_solution(12394601980561422957)
XLA Ops:
  0.6 0.7 pad_bitcast_fusion.2
  1.3 0.7 pad_bitcast_fusion
  2.0 1.9 concatenate.3.pack
  3.9 1.6 copy.18
  5.4 3.7 %shard_map.163 = (f32[384,16]{1,0:T(8,128)}, f32[16,384]{1,0:T(8,128)}, f32[384,16]{1,0:T(8,128)}, f32[384,1]{1,0:T(8,128)}, f32[1,384]{1,0:T(1,128)}, /*index=5...) custom-call(f32[16,128]{1,0:T(8,128)} %concatenate.3.pack, f32[384,16]{1,0:T(8,128)} %bitcast.50, ...), custom_call_target="tpu_custom_call" | custom-call | tf_op jit(solution)/shard_map/pallas_call | solution.py:641
  9.1 33.8 %shard_map.164 = (bf16[32,32,1024]{2,1,0:T(8,128)(2,1)}, bf16[8,16,1024]{2,1,0:T(8,128)(2,1)}, f32[8,1,1024]{2,1,0:T(1,128)}) custom-call(bf16[32,1024]{1,0:T(8,128)(2,1)} %get-tuple-element.55.rows_b, bf16[8,16,1024]{2,1,0:T(8,128)(2,1)} %bitcast.70, f32[1,1024]{1,0:T(1,128)} %get-tuple-element.57.carry), custom_call_target="tpu_custom_call" | custom-call | tf_op jit(solution)/shard_map/pallas_call | solution.py:641
  42.9 13.3 %shard_map.165 = (bf16[1024,1024]{1,0:T(8,128)(2,1)}, bf16[128,1024]{1,0:T(8,128)(2,1)}, f32[384,16]{1,0:T(8,128)}, f32[384,16]{1,0:T(8,128)}, f32[8,1024]{1,0:T(8,128)}, /*index=5*/f32[1,1]{1,0:T(1,128)}) custom-call(s32[4]{0:T(128)} %counts.3, f32[16,128]{1,0:T(8,128)} %concatenate.3.pack, f32[384,16]{1,0:T(8,128)} %get-tuple-element.50.sums, ...), custom_call_target="tpu_custom_call" | custom-call | tf_op jit(solution)/shard_map/pallas_call | solution.py:641
  56.2 27.4 %shard_map.166 = (f32[32,1024]{1,0:T(8,128)}, bf16[8,16,1024]{2,1,0:T(8,128)(2,1)}) custom-call(bf16[32,32,1024]{2,1,0:T(8,128)(2,1)} %bitcast.60, bf16[8,16,1024]{2,1,0:T(8,128)(2,1)} %bitcast.68, f32[8,1,1024]{2,1,0:T(1,128)} %get-tuple-element.62.carries), custom_call_target="tpu_custom_call" | custom-call | tf_op jit(solution)/shard_map/pallas_call | solution.py:641
  83.6 5.2 %shard_map.167.part = f32[16,128]{1,0:T(8,128)} custom-call(f32[16,128]{1,0:T(8,128)} %concatenate.3.pack, f32[384,16]{1,0:T(8,128)} %bitcast.51, f32[384,16]{1,0:T(8,128)} %get-tuple-element.50.sums, f32[384,16]{1,0:T(8,128)} %get-tuple-element.51.width, f32[384,1]{1,0:T(8,128)} %get-tuple-element.52.seg_c, bf16[384,1024]{1,0:T(8,128)(2,1)} %bitcast.40, ...), custom_call_target="tpu_custom_call" | custom-call | tf_op jit(solution)/shard_map/pallas_call | solution.py:641
  88.8 13.6 %shard_map.168 = (f32[16,128]{1,0:T(8,128)}, f32[32,1024]{1,0:T(8,128)}, f32[1,128]{1,0:T(1,128)}) custom-call(f32[16,128]{1,0:T(8,128)} %shard_map.167.part, f32[16,128]{1,0:T(8,128)} %concatenate.3.pack, f32[32,1024]{1,0:T(8,128)} %rows.3, f32[32,1024]{1,0:T(8,128)} %get-tuple-element.68.grad_rows), custom_call_target="tpu_custom_call" | custom-call | tf_op jit(solution)/shard_map/pallas_call | solution.py:641
  102.4 3.7 %shard_map.169 = (f32[384,16]{1,0:T(8,128)}, f32[16,384]{1,0:T(8,128)}, f32[384,16]{1,0:T(8,128)}, f32[384,1]{1,0:T(8,128)}, f32[1,384]{1,0:T(1,128)}, /*index=5...) custom-call(f32[16,128]{1,0:T(8,128)} %get-tuple-element.70.pack, f32[384,16]{1,0:T(8,128)} %bitcast.52, ...), custom_call_target="tpu_custom_call" | custom-call | tf_op jit(solution)/shard_map/pallas_call | solution.py:641
  106.1 29.0 %shard_map.170 = (bf16[32,32,1024]{2,1,0:T(8,128)(2,1)}, bf16[8,16,1024]{2,1,0:T(8,128)(2,1)}, f32[8,1,1024]{2,1,0:T(1,128)}) custom-call(bf16[32,1024]{1,0:T(8,128)(2,1)} %get-tuple-element.77.rows_b, bf16[8,16,1024]{2,1,0:T(8,128)(2,1)} %bitcast.71, f32[1,1024]{1,0:T(1,128)} %get-tuple-element.79.carry), custom_call_target="tpu_custom_call" | custom-call | tf_op jit(solution)/shard_map/pallas_call | solution.py:641
  135.2 13.3 %shard_map.171 = (bf16[1024,1024]{1,0:T(8,128)(2,1)}, bf16[128,1024]{1,0:T(8,128)(2,1)}, f32[384,16]{1,0:T(8,128)}, f32[384,16]{1,0:T(8,128)}, f32[8,1024]{1,0:T(8,128)}, /*index=5*/f32[1,1]{1,0:T(1,128)}) custom-call(s32[4]{0:T(128)} %counts.3, f32[16,128]{1,0:T(8,128)} %get-tuple-element.70.pack, f32[384,16]{1,0:T(8,128)} %get-tuple-element.72.sums, ...), custom_call_target="tpu_custom_call" | custom-call | tf_op jit(solution)/shard_map/pallas_call | solution.py:641
  148.4 27.3 %shard_map.172 = (f32[32,1024]{1,0:T(8,128)}, bf16[8,16,1024]{2,1,0:T(8,128)(2,1)}) custom-call(bf16[32,32,1024]{2,1,0:T(8,128)(2,1)} %bitcast.61, bf16[8,16,1024]{2,1,0:T(8,128)(2,1)} %bitcast.69, f32[8,1,1024]{2,1,0:T(1,128)} %get-tuple-element.84.carries), custom_call_target="tpu_custom_call" | custom-call | tf_op jit(solution)/shard_map/pallas_call | solution.py:641
  175.8 0.0 copy-start
  175.8 5.2 %shard_map.173.part = f32[16,128]{1,0:T(8,128)} custom-call(f32[16,128]{1,0:T(8,128)} %get-tuple-element.70.pack, f32[384,16]{1,0:T(8,128)} %bitcast.53, f32[384,16]{1,0:T(8,128)} %get-tuple-element.72.sums, f32[384,16]{1,0:T(8,128)} %get-tuple-element.73.width, f32[384,1]{1,0:T(8,128)} %get-tuple-element.74.seg_c, bf16[384,1024]{1,0:T(8,128)(2,1)} %bitcast.43, ...), custom_call_target="tpu_custom_call" | custom-call | tf_op jit(solution)/shard_map/pallas_call | solution.py:641
  181.0 14.3 %shard_map.174 = (f32[16,128]{1,0:T(8,128)}, f32[32,1024]{1,0:T(8,128)}, f32[1,128]{1,0:T(1,128)}) custom-call(f32[16,128]{1,0:T(8,128)} %shard_map.173.part, f32[16,128]{1,0:T(8,128)} %get-tuple-element.70.pack, f32[32,1024]{1,0:T(8,128)} %get-tuple-element.71.rows, f32[32,1024]{1,0:T(8,128)} %get-tuple-element.90.grad_rows), custom_call_target="tpu_custom_call" | custom-call | tf_op jit(solution)/shard_map/pallas_call | solution.py:641
  195.3 0.0 copy-done
  195.3 1.2 pad_maximum_fusion
  196.5 1.3 slice_bitcast_fusion.1
  197.8 1.3 slice_bitcast_fusion
  199.1 1.6 copy.23
  (1 shorter events, 0.0 us)
Async XLA Ops:
  175.8 19.5 %copy-start = (f32[1,128]{1,0:T(1,128)S(1)}, f32[1,128]{1,0:T(1,128)}, u32[]{:S(2)}) copy-start(f32[1,128]{1,0:T(1,128)} %get-tuple-element.69) | copy-start | bytes 1540

commit v3 on v2

--- a/solution.py
+++ b/solution.py
@@ -62,8 +62,8 @@
     return width // LANES
 
 
-def state_kernel(
-    pack, raw, raw_t, ids_r, x, proj, rows, sums, sums_t, width, seg_c, seg_r, state, carry, rows_b
+def state_part(
+    pack, raw, raw_t, ids_r, x, proj, sums, sums_t, width, seg_c, seg_r, state, carry
 ):
     tokens, heads = raw.shape
     inner = x.shape[1]
@@ -84,7 +84,6 @@
     stop = jnp.where(ids_r[...] == 0, 1.0, 0.0)
     sc = jnp.sum(jnp.where(i >= j, stop, 0.0), axis=1, keepdims=True)
     sr = jnp.sum(jnp.where(i <= j, column(stop), 0.0), axis=0, keepdims=True)
-    rows_b[...] = rows[...].astype(bf16)
     seg_c[...] = sc
     seg_r[...] = sr
     last = sc[tokens - 1 : tokens, :]
@@ -92,9 +91,12 @@
     tail = jnp.where(sc == last, jnp.exp(final - s), 0.0)
     weighted = (x[...].astype(f32) * spread(w * tail, ones)).astype(bf16)
     b = proj[:, : proj.shape[1] // 2]
-    state[...] = lax.dot_general(
+    ended = lax.dot_general(
         b, weighted, (((0,), (0,)), ((), ())), preferred_element_type=f32
-    ).astype(bf16)
+    )
+    piece = state.shape[1]
+    for p in range(state.shape[0]):
+        state[p] = ended[p * piece : (p + 1) * piece].astype(bf16)
     kept = jnp.where(last == 0.0, jnp.exp(final), 0.0)
     carry[...] = spread(jnp.broadcast_to(kept, (8, heads)), ones)[0:1, :]
 
@@ -187,9 +189,9 @@
     col_dot[...] = head_sum(prod[...], ones)
 
 
-def back_kernel(
+def back_part(
     pack, raw, sums, width, seg_c, x, proj, after, state, carry, row_dot, col_dot, small, loss,
-    grad_rows, out,
+    out,
 ):
     tokens, heads = sums.shape
     inner = x.shape[1]
@@ -203,8 +205,9 @@
     last = sc[tokens - 1 : tokens, :]
     final = s[tokens - 1 : tokens, :]
     tail = jnp.where(sc == last, jnp.exp(final - s), 0.0)
-    pulled = head_sum(dot(proj[:, : proj.shape[1] // 2], after[...]) * x[...].astype(f32), ones) * tail
-    moved = after[...].astype(f32) * state[...].astype(f32)
+    after = jnp.concatenate([after[p].astype(f32) for p in range(after.shape[0])], axis=0)
+    pulled = head_sum(dot(proj[:, : proj.shape[1] // 2], after.astype(bf16)) * x[...].astype(f32), ones) * tail
+    moved = after * state[...].astype(f32)
     both = jnp.concatenate(
         [
             jnp.sum(moved, axis=0, keepdims=True) * carry[...],
@@ -221,8 +224,6 @@
     j = lax.broadcasted_iota(jnp.int32, (tokens, tokens), 1)
     d_rate = dot((i <= j).astype(f32), d_sums, precision=highest) + d_final
     d_width = (col + rate_row * d_rate) * jax.nn.sigmoid(raw[...] + bias_row)
-    rows = grad_rows[...]
-    square = jnp.sum(jnp.sum(rows * rows, axis=1, keepdims=True), axis=0, keepdims=True)
     out[...] = jnp.zeros(out.shape, f32)
     for k in range(g):
         out[k : k + 1, :] = small[0:1, k * LANES : (k + 1) * LANES]
@@ -230,7 +231,6 @@
     out[g + 1 : g + 2, :heads] = jnp.sum(d_width, axis=0, keepdims=True)
     out[g + 2 : g + 3, :heads] = both[1:2, :]
     out[g + 3 : g + 4, :] = jnp.broadcast_to(loss[...], (1, LANES))
-    out[g + 4 : g + 5, :] = jnp.broadcast_to(square, (1, LANES))
 
 
 class Spot:
@@ -297,13 +297,13 @@
 
 
 def gather_kernel(
-    n_dp, n_seq, rows_b, state, carry, full, entering, carries,
-    landed, ready, own_sem, w_recv, high_send, low_send, y_send, core_send,
+    n_dp, n_seq, pack, raw, raw_t, ids_r, x, proj, rows,
+    sums, sums_t, width, seg_c, seg_r, carry, full, entering, carries,
+    state, landed, ready, w_recv, high_send, low_send, y_send, core_send,
     s_send, s_recv, c_send, c_recv, r_send, r_recv,
 ):
     at = Spot(n_dp, n_seq)
-    own = pltpu.make_async_copy(rows_b, full.at[at.me], own_sem)
-    own.start()
+    full[at.me] = rows[...].astype(bf16)
     at.meet(True)
     mine = at.seq
     back = lambda t: (mine + n_seq - t) % n_seq
@@ -361,10 +361,12 @@
         lead(t).start()
         first(t).start()
 
-    each(n_seq, start)
-    own.wait()
     each(at.highs, lambda t: high_edge(t).start())
     onward(at.y, at.seq, True, True)
+    state_part(
+        pack, raw, raw_t, ids_r, x, proj, sums, sums_t, width, seg_c, seg_r, state, carry
+    )
+    each(n_seq, start)
     carries[mine] = carry[...]
     landed[mine] = state[mine]
 
@@ -442,10 +444,12 @@
 
 
 def scatter_kernel(
-    n_dp, n_seq, grad, state, carries, total, leaving,
+    n_dp, n_seq, grad, state, carries, pack, raw, sums, width, seg_c, x, proj, entering, carry,
+    row_dot, col_dot, small, loss_part, rows, new_pack, new_rows, loss,
+    part, leaving, by_core, by_y, by_low, by_high,
     staged, from_core, from_y, from_low, from_high, landed, ready,
     core_send, core_recv, y_send, y_recv, low_send, low_recv, high_send, high_recv,
-    s_send, s_recv, r_send, r_recv,
+    s_send, s_recv, r_send, r_recv, send, recv,
 ):
     at = Spot(n_dp, n_seq)
     at.meet(True)
@@ -553,6 +557,11 @@
             running = carries[d] * running + landed[d].astype(f32)
     each(n_seq, lambda t: second(t).start())
     leaving[mine] = ready[mine]
+    each(n_seq, lambda t: second_in(t).wait_recv())
+    back_part(
+        pack, raw, sums, width, seg_c, x, proj, leaving, entering, carry, row_dot, col_dot,
+        small, loss_part, part,
+    )
 
     def to_low(t):
         def one(u):
@@ -575,8 +584,38 @@
     for t in range(1, at.highs):
         high_edge(t).wait_recv()
         acc = acc + from_high[t].astype(f32)
-    total[...] = acc
-    each(n_seq, lambda t: second_in(t).wait_recv())
+    g = gain_rows(x.shape[1])
+    square = jnp.sum(jnp.sum(acc * acc, axis=1, keepdims=True), axis=0, keepdims=True)
+    place = lax.broadcasted_iota(jnp.int32, part.shape, 0)
+    summed = jnp.where(place == g + 4, square, part[...])
+    levels = [
+        (by_core, at.cores, at.core, at.core_peer),
+        (by_y, at.ys, at.y, at.y_peer),
+        (by_low, at.lows, at.low, at.low_peer),
+        (by_high, at.highs, at.high, at.high_peer),
+    ]
+    base = 0
+    for held, count, digit, peer in levels:
+        held[digit] = summed
+
+        def edge(t, slot, held=held, digit=digit, peer=peer, base=base):
+            return remote(held.at[digit], held.at[slot], send.at[base + t], recv.at[base + t], peer(t))
+
+        each(count, lambda t: edge(t, digit).start())
+        each(count, lambda t: edge(t, (digit + count - t) % count).wait_recv())
+        summed = held[0]
+        for k in range(1, count):
+            summed = summed + held[k]
+        each(count, lambda t: edge(t, digit).wait_send())
+        base += count
+    row = lax.broadcasted_iota(jnp.int32, summed.shape, 0)
+    grads = jnp.where(row < g + 3, summed, 0.0)
+    lane_sum = jnp.sum(grads * grads, axis=0, keepdims=True)
+    norm_square = jnp.sum(lane_sum, axis=1, keepdims=True) + summed[g + 4 : g + 5, 0:1]
+    factor = clip_limit / jnp.maximum(jnp.sqrt(norm_square), clip_limit)
+    new_pack[...] = pack[...] - learn_rate * factor * grads
+    new_rows[...] = rows[...] - learn_rate * factor * acc
+    loss[...] = summed[g + 3 : g + 4, :]
 
     def sent(t):
         first(t).wait_send()
@@ -592,44 +631,6 @@
             at.ys * n_seq, lambda k: core_edge(t, k // n_seq, k % n_seq).wait_send(), 0
         ),
     )
-
-
-def update_kernel(
-    n_dp, n_seq, inner, part, pack, rows, grad_rows, new_pack, new_rows, loss,
-    by_core, by_y, by_low, by_high, send, recv,
-):
-    at = Spot(n_dp, n_seq)
-    at.meet(False)
-    summed = part[...]
-    levels = [
-        (by_core, at.cores, at.core, at.core_peer),
-        (by_y, at.ys, at.y, at.y_peer),
-        (by_low, at.lows, at.low, at.low_peer),
-        (by_high, at.highs, at.high, at.high_peer),
-    ]
-    base = 0
-    for held, count, digit, peer in levels:
-        held[digit] = summed
-
-        def edge(t, slot, held=held, digit=digit, peer=peer, base=base):
-            return remote(held.at[digit], held.at[slot], send.at[base + t], recv.at[base + t], peer(t))
-
-        each(count, lambda t: edge(t, digit).start())
-        each(count, lambda t: edge(t, (digit + count - t) % count).wait_recv())
-        summed = held[0]
-        for k in range(1, count):
-            summed = summed + held[k]
-        each(count, lambda t: edge(t, digit).wait_send())
-        base += count
-    g = gain_rows(inner)
-    row = lax.broadcasted_iota(jnp.int32, summed.shape, 0)
-    grads = jnp.where(row < g + 3, summed, 0.0)
-    lane_sum = jnp.sum(grads * grads, axis=0, keepdims=True)
-    norm_square = jnp.sum(lane_sum, axis=1, keepdims=True) + summed[g + 4 : g + 5, 0:1]
-    factor = clip_limit / jnp.maximum(jnp.sqrt(norm_square), clip_limit)
-    new_pack[...] = pack[...] - learn_rate * factor * grads
-    new_rows[...] = rows[...] - learn_rate * factor * grad_rows[...]
-    loss[...] = summed[g + 3 : g + 4, :]
 
 
 def call(body, outs, scratch=(), collective=None):
@@ -694,30 +695,21 @@
     losses = []
     per_head = ((tokens, heads), f32)
     for _ in range(STEPS):
-        sums, sums_t, width, seg_c, seg_r, state, carry, rows_b = call(
-            state_kernel,
+        sums, sums_t, width, seg_c, seg_r, carry, full, entering, carries = call(
+            functools.partial(gather_kernel, n_dp, n_seq),
             [
                 per_head,
                 ((heads, tokens), f32),
                 per_head,
                 ((tokens, 1), f32),
                 ((1, tokens), f32),
-                ((ns, inner), bf16),
                 ((1, inner), f32),
-                ((share, model), bf16),
-            ],
-        )(pack, raw, raw_t, ids_r, x, proj, rows)
-        full, entering, carries = call(
-            functools.partial(gather_kernel, n_dp, n_seq),
-            [
                 ((n, share, model), bf16),
                 ((n_seq, piece, inner), bf16),
                 ((n_seq, 1, inner), f32),
             ],
-            [
-                pltpu.VMEM((n_seq, piece, inner), bf16),
-                pltpu.VMEM((n_seq, piece, inner), bf16),
-                dma,
+            [pltpu.VMEM((n_seq, piece, inner), bf16)] * 3
+            + [
                 dma((n,)),
                 dma((n_seq,)),
                 dma((n_seq * n_seq,)),
@@ -726,7 +718,7 @@
             ]
             + [dma((n_seq,))] * 6,
             0,
-        )(rows_b, state.reshape(n_seq, piece, inner), carry)
+        )(pack, raw, raw_t, ids_r, x, proj, rows)
         weight = full.reshape(n * share, model)
         entering = entering.reshape(ns, inner)
         weight_grad, state_grad, row_dot, col_dot, small, loss = call(
@@ -749,41 +741,24 @@
             token_counts, pack, sums, sums_t, width, seg_c, seg_r, x, z, proj, target, weight,
             entering,
         )
-        grad_rows, after = call(
+        pack, rows, loss_row = call(
             functools.partial(scatter_kernel, n_dp, n_seq),
-            [((share, model), f32), ((n_seq, piece, inner), bf16)],
-            [
-                pltpu.VMEM((n, share, model), bf16),
-                pltpu.VMEM((n, share, model), bf16),
-                pltpu.VMEM((n, share, model), bf16),
-                pltpu.VMEM((n_seq, share, model), bf16),
-                pltpu.VMEM((n_seq, share, model), bf16),
-                pltpu.VMEM((n_seq, piece, inner), bf16),
-                pltpu.VMEM((n_seq, piece, inner), bf16),
-            ]
+            [((pack_rows, LANES), f32), ((share, model), f32), ((1, LANES), f32)],
+            [pltpu.VMEM((pack_rows, LANES), f32), pltpu.VMEM((n_seq, piece, inner), bf16)]
+            + [pltpu.VMEM((k, pack_rows, LANES), f32) for k in (n_dp, n_dp, n_seq, n_seq)]
+            + [pltpu.VMEM((n, share, model), bf16)] * 3
+            + [pltpu.VMEM((n_seq, share, model), bf16)] * 2
+            + [pltpu.VMEM((n_seq, piece, inner), bf16)] * 2
             + [dma((n,))] * 4
-            + [dma((n_seq,))] * 8,
+            + [dma((n_seq,))] * 8
+            + [dma((n,))] * 2,
             1,
         )(
             weight_grad.reshape(n, share, model),
             state_grad.reshape(n_seq, piece, inner),
-            carries,
+            carries, pack, raw, sums, width, seg_c, x, proj, entering, carry, row_dot, col_dot,
+            small, loss, rows,
         )
-        part = call(back_kernel, [((pack_rows, LANES), f32)])(
-            pack, raw, sums, width, seg_c, x, proj, after.reshape(ns, inner), entering, carry,
-            row_dot, col_dot, small, loss, grad_rows,
-        )[0]
-        pack, rows, loss_row = call(
-            functools.partial(update_kernel, n_dp, n_seq, inner),
-            [
-                ((pack_rows, LANES), f32),
-                ((share, model), f32),
-                ((1, LANES), f32),
-            ],
-            [pltpu.VMEM((k, pack_rows, LANES), f32) for k in (n_dp, n_dp, n_seq, n_seq)]
-            + [dma((n,))] * 2,
-            2,
-        )(part, pack, rows, grad_rows)
         losses.append(loss_row[0, 0])
     return (
         jnp.stack(losses),

time: 201 us -> 186 us (0.925)
  Pallas kernels: 190 us -> 175 us
    pallas_call x12 -> x6, Pallas kernels: 190 us -> 175 us  [run(): pl.pallas_call(body, out_shape=tuple((jax.ShapeDtypeStruct(*o) for o in o...]
where the time goes in v3:
time: 186 us
  Pallas kernels  175 us (94%)
  local copies, waits for them, and re-layouts  8.94 us (5%)
    pallas_call x6, Pallas kernels, run(): pl.pallas_call(body, out_shape=tuple((jax.ShapeDtypeStruct(*o) for o in o...  175 us

profile of v3, /device:TPU:0, one launch (start us, length us, event | category | flops | bytes accessed | tf_op | source)
XLA Modules:
  0.0 185.9 jit_solution(13988341472279615315)
XLA Ops:
  0.6 0.7 pad_bitcast_fusion.2
  1.3 0.7 pad_bitcast_fusion
  2.0 1.9 %concatenate.3.pack = f32[16,128]{1,0:T(8,128)} concatenate(f32[8,128]{1,0:T(8,128)} %bitcast.66, f32[1,128]{1,0:T(1,128)S(1)} %pad_bitcast_fusion.2, f32[1,128]{1,0:T(1,128)S(1)} %get-tuple-element.82, f32[1,128]{1,0:T(1,128)S(1)} %get-tuple-element.81, f32[5,128]{1,0:T(8,128)S(1)} %broadcast_in_dim.15), dimensions={0} | concatenate | bytes 16384 | tf_op jit(solution)/shard_map/concatenate | solution.py:684
  3.8 1.6 copy.18
  5.4 32.2 %shard_map.163 = (f32[384,16]{1,0:T(8,128)}, f32[16,384]{1,0:T(8,128)}, f32[384,16]{1,0:T(8,128)}, f32[384,1]{1,0:T(8,128)}, f32[1,384]{1,0:T(1,128)}, /*index=5...) custom-call(f32[16,128]{1,0:T(8,128)} %concatenate.3.pack, ...), custom_call_target="tpu_custom_call" | custom-call | tf_op jit(solution)/shard_map/pallas_call | solution.py:642
  37.7 13.3 %shard_map.164 = (bf16[1024,1024]{1,0:T(8,128)(2,1)}, bf16[128,1024]{1,0:T(8,128)(2,1)}, f32[384,16]{1,0:T(8,128)}, f32[384,16]{1,0:T(8,128)}, f32[8,1024]{1,0:T(8,128)}, /*index=5*/f32[1,1]{1,0:T(1,128)}) custom-call(s32[4]{0:T(128)} %counts.3, f32[16,128]{1,0:T(8,128)} %concatenate.3.pack, f32[384,16]{1,0:T(8,128)} %get-tuple-element.42.sums, ...), custom_call_target="tpu_custom_call" | custom-call | tf_op jit(solution)/shard_map/pallas_call | solution.py:642
  50.9 43.8 %shard_map.165 = (f32[16,128]{1,0:T(8,128)}, f32[32,1024]{1,0:T(8,128)}, f32[1,128]{1,0:T(1,128)}) custom-call(bf16[32,32,1024]{2,1,0:T(8,128)(2,1)} %bitcast.57, bf16[8,16,1024]{2,1,0:T(8,128)(2,1)} %bitcast.63, f32[8,1,1024]{2,1,0:T(1,128)} %get-tuple-element.51.carries, f32[16,128]{1,0:T(8,128)} %concatenate.3.pack, f32[384,16]{1,0:T(8,128)} %bitcast.47, ...), custom_call_target="tpu_custom_call" | custom-call | tf_op jit(solution)/shard_map/pallas_call | solution.py:642
  94.7 27.6 %shard_map.166 = (f32[384,16]{1,0:T(8,128)}, f32[16,384]{1,0:T(8,128)}, f32[384,16]{1,0:T(8,128)}, f32[384,1]{1,0:T(8,128)}, f32[1,384]{1,0:T(1,128)}, /*index=5...) custom-call(f32[16,128]{1,0:T(8,128)} %get-tuple-element.58.pack, ...), custom_call_target="tpu_custom_call" | custom-call | tf_op jit(solution)/shard_map/pallas_call | solution.py:642
  122.3 13.3 %shard_map.167 = (bf16[1024,1024]{1,0:T(8,128)(2,1)}, bf16[128,1024]{1,0:T(8,128)(2,1)}, f32[384,16]{1,0:T(8,128)}, f32[384,16]{1,0:T(8,128)}, f32[8,1024]{1,0:T(8,128)}, /*index=5*/f32[1,1]{1,0:T(1,128)}) custom-call(s32[4]{0:T(128)} %counts.3, f32[16,128]{1,0:T(8,128)} %get-tuple-element.58.pack, f32[384,16]{1,0:T(8,128)} %get-tuple-element.60.sums, ...), custom_call_target="tpu_custom_call" | custom-call | tf_op jit(solution)/shard_map/pallas_call | solution.py:642
  135.5 0.0 copy-start
  135.5 45.0 %shard_map.168 = (f32[16,128]{1,0:T(8,128)}, f32[32,1024]{1,0:T(8,128)}, f32[1,128]{1,0:T(1,128)}) custom-call(bf16[32,32,1024]{2,1,0:T(8,128)(2,1)} %bitcast.56, bf16[8,16,1024]{2,1,0:T(8,128)(2,1)} %bitcast.62, f32[8,1,1024]{2,1,0:T(1,128)} %get-tuple-element.69.carries, f32[16,128]{1,0:T(8,128)} %get-tuple-element.58.pack, f32[384,16]{1,0:T(8,128)} %bitcast.49, ...), custom_call_target="tpu_custom_call" | custom-call | tf_op jit(solution)/shard_map/pallas_call | solution.py:642
  180.6 0.0 copy-done
  180.6 1.2 pad_maximum_fusion
  181.8 1.3 slice_bitcast_fusion.1
  183.1 1.3 slice_bitcast_fusion
  184.4 1.6 copy.23
  (1 shorter events, 0.0 us)
Async XLA Ops:
  135.5 45.0 %copy-start = (f32[1,128]{1,0:T(1,128)S(1)}, f32[1,128]{1,0:T(1,128)}, u32[]{:S(2)}) copy-start(f32[1,128]{1,0:T(1,128)} %get-tuple-element.57) | copy-start | bytes 1540
